TPU v7x, 32 devices: a whole 2x2x4 slice. The times are simulated.
32 devices in a mesh: dp: 16 (over z, y, x), tensor: 2 (over core).
Axes of the slice: x: 2, y: 2, z: 4, core: 2. Of those that a mesh axis runs over, the one named last changes fastest.
Arguments:
- encoded: bfloat16 [8192, 1152], P('dp', 'tensor'), may hold values from -9 to 9
- counts: int32 [128], P('dp'), may hold values from 16 to 64
- win_ids: int32 [128, 64], P('dp'), may hold values from 0 to 31, never falling along the last dimension, each value on 1 to 8 neighbouring positions
- dest_seq: int32 [128], P('dp'), may hold values from 0 to 15, as said below
- dest_slot: int32 [128], P('dp'), may hold values from 0 to 7, as said below
- w_first: bfloat16 [1152, 4608], P(None, 'tensor'), may hold values from -0.3125 to 0.3125
- b_first: float32 [4608], P('tensor'), may hold values from -3 to 3
- w_second: bfloat16 [4608, 2304], P('tensor'), may hold values from -0.1875 to 0.1875
- b_second: float32 [2304], P('tensor'), may hold values from -3 to 3
Outputs:
- projected: bfloat16 [4096, 2304], P('dp', 'tensor')
Inputs may be any that keep to these rules, and one draw needn't show every extreme that they name: `dest_seq`: every sequence receives exactly 8 samples, no two of them from the same index of dp. `dest_slot`: the samples that one sequence receives have distinct block offsets.
All inputs are finite; a program needn't handle non-finite values.
Results may differ from a plain program's by a relative error of at most 0.009.
Values may be sent and summed in bfloat16 or wider, within the bound.
No kernel may reach another device: no remote copies, remote signals or barrier semaphores. Data moves between devices by JAX's collectives and lax.ppermute only.
A program may use at most 128 MiB of HBM per device.

v0:
```python
import jax
import jax.numpy as jnp
from jax import lax
from jax.sharding import PartitionSpec as P

BLOCK = 32


def pool_blocks(ids_live, tokens):
    windows = jnp.arange(BLOCK, dtype=jnp.int32)
    onehot = ids_live[:, None, :] == windows[None, :, None]
    number = jnp.sum(onehot.astype(jnp.float32), axis=2)
    totals = jnp.einsum(
        "nwc,ncf->nwf", onehot.astype(jnp.bfloat16), tokens, preferred_element_type=jnp.float32
    )
    return (totals / jnp.maximum(number, 1.0)[:, :, None]).astype(jnp.bfloat16)


def shards(encoded, counts, win_ids, dest_seq, dest_slot, w_first, b_first, w_second, b_second):
    samples = counts.shape[0]
    capacity = win_ids.shape[1]
    tokens = encoded.reshape(samples, capacity, encoded.shape[1])
    positions = jnp.arange(capacity, dtype=jnp.int32)
    ids_live = jnp.where(positions[None, :] < counts[:, None], win_ids, -1)
    groups = lax.axis_size("dp")
    targets = jnp.arange(groups, dtype=jnp.int32)
    chosen = dest_seq[None, :] == targets[:, None]
    picker = chosen.astype(jnp.bfloat16)
    offset_plus = jnp.sum(jnp.where(chosen, dest_slot[None, :] + 1, 0), axis=1)[:, None]
    pooled = pool_blocks(ids_live, tokens)
    outgoing = jnp.einsum("es,swf->ewf", picker, pooled, preferred_element_type=jnp.float32).astype(
        jnp.bfloat16
    )
    arrived, got_offset = (
        lax.all_to_all(outgoing, "dp", split_axis=0, concat_axis=0, tiled=True),
        lax.all_to_all(
            offset_plus.astype(jnp.bfloat16), "dp", split_axis=0, concat_axis=0, tiled=True
        ),
    )
    got_offset = got_offset.astype(jnp.int32)
    slot_from = got_offset[:, 0] - 1
    slot_ids = jnp.arange(samples, dtype=jnp.int32)
    placer = (slot_from[None, :] == slot_ids[:, None]).astype(jnp.bfloat16)
    packed = jnp.einsum("kd,dwf->kwf", placer, arrived, preferred_element_type=jnp.float32).astype(
        jnp.bfloat16
    )
    packed = packed.reshape(samples * arrived.shape[1], arrived.shape[2])
    preact = (
        jnp.dot(
            lax.all_gather(packed, "tensor", axis=1, tiled=True),
            w_first,
            preferred_element_type=jnp.float32,
        )
        + b_first
    )
    hidden = jax.nn.gelu(preact, approximate=True).astype(jnp.bfloat16)
    partial_value = jnp.dot(hidden, w_second, preferred_element_type=jnp.float32)
    summed = lax.psum_scatter(
        partial_value.astype(jnp.bfloat16), "tensor", scatter_dimension=1, tiled=True
    ).astype(jnp.float32)
    return (summed + b_second).astype(jnp.bfloat16)


def solution(mesh):
    placed = (
        P("dp", "tensor"),
        P("dp"),
        P("dp", None),
        P("dp"),
        P("dp"),
        P(None, "tensor"),
        P("tensor"),
        P("tensor", None),
        P("tensor"),
    )
    return jax.shard_map(
        shards, mesh=mesh, in_specs=placed, out_specs=P("dp", "tensor"), check_vma=False
    )
```

profile of v0, /device:TPU:0, one launch (start us, length us, event | category | flops | bytes accessed | tf_op | source)
XLA Modules:
  0.0 76.2 jit_solution(11469393669298495190)
XLA Ops:
  6.5 0.0 copy-start.1
  6.5 0.7 broadcast_add_fusion
  7.2 0.7 select_reduce_fusion
  8.0 0.7 copy.19
  8.7 8.3 %all-to-all-start = ((bf16[16,1,1]{2,1,0:T(2,128)(2,1)}), bf16[16,1,1]{2,1,0:T(2,128)(2,1)S(1)}, u32[]{:S(2)}, u32[]{:S(2)}) async-start(bf16[16,1,1]{2,1,0:T(2,128)(2,1)} %copy.19), calls=%async_computation | async-start | bytes 16384 | tf_op jit(solution)/shard_map/all_to_all | solution.py:36
  17.0 0.8 fusion.16
  17.8 0.1 convert_reduce_fusion
  17.9 1.4 %copy.20 = bf16[512,576]{1,0:T(8,128)(2,1)S(1)} copy(bf16[512,576]{0,1:T(8,128)(2,1)} %param.9) | data formatting | bytes 1179648 | tf_op args[0]
  19.3 0.2 fusion.8
  19.5 0.0 copy-done.1
  19.5 0.5 convolution_convert_fusion.1
  20.0 1.0 %copy.22 = bf16[16,32,576]{2,1,0:T(8,128)(2,1)} copy(bf16[16,32,576]{2,0,1:T(8,128)(2,1)S(1)} %convolution_convert_fusion.1) | data formatting | bytes 1179648 | tf_op jit(solution)/shard_map/convert_element_type | solution.py:31
  20.9 0.0 copy-start.2
  20.9 3.3 %all-to-all-done = bf16[16,1,1]{2,1,0:T(2,128)(2,1)S(1)} async-done(((bf16[16,1,1]{2,1,0:T(2,128)(2,1)}), bf16[16,1,1]{2,1,0:T(2,128)(2,1)S(1)}, u32[]{:S(2)}, u32[]{:S(2)}) %all-to-all-start) | async-done | bytes 64 | tf_op jit(solution)/shard_map/all_to_all | solution.py:36
  24.2 3.7 %all-to-all-start.1 = ((bf16[16,32,576]{2,1,0:T(8,128)(2,1)}), bf16[16,32,576]{2,1,0:T(8,128)(2,1)S(1)}, u32[]{:S(2)}, u32[]{:S(2)}) async-start(bf16[16,32,576]{2,1,0:T(8,128)(2,1)} %copy.22), calls=%async_computation.1 | async-start | bytes 1310720 | tf_op jit(solution)/shard_map/all_to_all | solution.py:35
  28.0 0.0 reduce-scatter.4.cloned.1.call-start
  28.0 0.4 add_reduce_fusion
  28.4 16.4 %all-to-all-done.1 = bf16[16,32,576]{2,1,0:T(8,128)(2,1)S(1)} async-done(((bf16[16,32,576]{2,1,0:T(8,128)(2,1)}), bf16[16,32,576]{2,1,0:T(8,128)(2,1)S(1)}, u32[]{:S(2)}, u32[]{:S(2)}) %all-to-all-start.1) | async-done | bytes 589856 | tf_op jit(solution)/shard_map/all_to_all | solution.py:35
  44.8 0.3 convolution_convert_fusion.2
  45.1 0.2 copy.25
  45.3 2.2 %all_gather.3 = bf16[256,1152]{0,1:T(8,128)(2,1)S(1)} all-gather(bf16[256,576]{0,1:T(8,128)(2,1)S(1)} %copy.25), channel_id=1, replica_groups=mesh['dp'=16,'tensor'=2] {'tensor'}, dimensions={1}, use_global_device_ids=true | all-gather | bytes 884736 | tf_op jit(solution)/shard_map/all_gather | solution.py:50
  47.5 0.0 copy-done.2
  47.5 10.6 %convolution_convert_fusion = bf16[256,2304]{1,0:T(8,128)(2,1)S(1)} fusion(bf16[2304,2304]{1,0:T(8,128)(2,1)} %param.16, bf16[256,1152]{0,1:T(8,128)(2,1)S(1)} %all_gather.3, bf16[1152,2304]{1,0:T(8,128)(2,1)} %param.14, f32[2304]{0:T(1024)S(1)} %copy-done.2), kind=kOutput, calls=%fused_computation.1 | convolution fusion | flops 4083351552 | bytes 17703936 | tf_op jit(solution)/shard_map/dot_general | solution.py:57
  58.1 0.0 copy-start
  58.2 1.4 %copy.26 = bf16[256,2304]{0,1:T(8,128)(2,1)} copy(bf16[256,2304]{1,0:T(8,128)(2,1)S(1)} %convolution_convert_fusion) | data formatting | bytes 2359296
  59.6 0.0 reduce-scatter.4.cloned.1.call-update
  59.6 7.5 %reduce-scatter.4.cloned.1.call-done = bf16[1152,256]{1,0:T(8,128)(2,1)} async-done(((bf16[2304,256]{1,0:T(8,128)(2,1)}), bf16[1152,256]{1,0:T(8,128)(2,1)}) %reduce-scatter.4.cloned.1.call-update) | async-done | bytes 589840
  67.1 1.4 %copy.27 = bf16[256,1152]{1,0:T(8,128)(2,1)S(1)} copy(bf16[256,1152]{0,1:T(8,128)(2,1)} %bitcast.19) | data formatting | bytes 1179648
  68.5 0.0 copy-done
  68.5 0.9 %add_convert_fusion = bf16[256,1152]{1,0:T(8,128)(2,1)} fusion(bf16[256,1152]{1,0:T(8,128)(2,1)S(1)} %copy.27, f32[1152]{0:T(1024)S(1)} %copy-done), kind=kLoop, calls=%fused_computation.15 | loop fusion | flops 884736 | bytes 1184256 | tf_op jit(solution)/shard_map/convert_element_type | solution.py:61
  (3 shorter events, 0.0 us)
Async XLA Ops:
  6.5 13.0 %copy-start.1 = (s32[8]{0:T(128)S(1)}, s32[8]{0:T(128)}, u32[]{:S(2)}) copy-start(s32[8]{0:T(128)} %param.12) | copy-start | bytes 100
  8.7 15.6 %all-to-all-start = ((bf16[16,1,1]{2,1,0:T(2,128)(2,1)}), bf16[16,1,1]{2,1,0:T(2,128)(2,1)S(1)}, u32[]{:S(2)}, u32[]{:S(2)}) async-start(bf16[16,1,1]{2,1,0:T(2,128)(2,1)} %copy.19), calls=%async_computation | async-start | bytes 16384 | tf_op jit(solution)/shard_map/all_to_all | solution.py:36
  20.9 26.6 %copy-start.2 = (f32[2304]{0:T(1024)S(1)}, f32[2304]{0:T(1024)}, u32[]{:S(2)}) copy-start(f32[2304]{0:T(1024)} %param.15) | copy-start | bytes 27652
  24.2 20.6 %all-to-all-start.1 = ((bf16[16,32,576]{2,1,0:T(8,128)(2,1)}), bf16[16,32,576]{2,1,0:T(8,128)(2,1)S(1)}, u32[]{:S(2)}, u32[]{:S(2)}) async-start(bf16[16,32,576]{2,1,0:T(8,128)(2,1)} %copy.22), calls=%async_computation.1 | async-start | bytes 1310720 | tf_op jit(solution)/shard_map/all_to_all | solution.py:35
  28.0 39.1 %reduce-scatter.4.cloned.1.call-start = ((), (), s32[]{:S(2)}) async-start(), calls=%async_computation.3 | async-start | bytes 1769472
  58.1 10.3 %copy-start = (f32[1152]{0:T(1024)S(1)}, f32[1152]{0:T(1024)}, u32[]{:S(2)}) copy-start(f32[1152]{0:T(1024)} %param.17) | copy-start | bytes 13828
Sparse Core Ops, SparseCore 0:
  59.7 7.3 reduce-scatter.3
where the time goes:
time: 76.7 us; the launch traced here: 76.2 us
  waiting for transfers between devices  27.2 us (35%)
  between operations  13.5 us (18%)
  starting transfers between devices  12.1 us (16%)
  matrix products  11.6 us (15%)
  local copies, waits for them, and re-layouts  6 us (8%)
  other arithmetic  3.59 us (5%)
  blocking collectives  2.23 us (3%)
    all_to_all x1, waiting for transfers between devices, shards(): lax.all_to_all(outgoing, 'dp', split_axis=0, concat_axis=0, tiled=True)  16.4 us
    dot_general x1, matrix products, shards(): jnp.dot(hidden, w_second, preferred_element_type=jnp.float32)  10.6 us
    all_to_all x1, starting transfers between devices, shards(): lax.all_to_all(offset_plus.astype(jnp.bfloat16), 'dp', split_axis=0, conc...  8.34 us
    unnamed x2, waiting for transfers between devices  7.54 us
    unnamed x9, local copies, waits for them, and re-layouts  4.15 us
    all_to_all x1, starting transfers between devices, shards(): lax.all_to_all(outgoing, 'dp', split_axis=0, concat_axis=0, tiled=True)  3.75 us
    all_to_all x1, waiting for transfers between devices, shards(): lax.all_to_all(offset_plus.astype(jnp.bfloat16), 'dp', split_axis=0, conc...  3.29 us
    all_gather x1, blocking collectives, shards(): lax.all_gather(packed, 'tensor', axis=1, tiled=True)  2.23 us
  transfers between devices with their start and end apart: 3, of which 3 were waited for; matrix products, arithmetic and copies ran while one was open for 6% of the time, Pallas kernels for 0%

commit v1 on v0

v1 whole, which is shorter than its diff:
```python
import functools

import jax
import jax.numpy as jnp
from jax import lax
from jax.experimental import pallas as pl
from jax.experimental.pallas import tpu as pltpu
from jax.sharding import PartitionSpec as P

BLOCK = 32
LANES = 128
HALF = LANES // 2
NOTE = 8
F32, BF16, I32 = jnp.float32, jnp.bfloat16, jnp.int32
VMEM = pl.BlockSpec(memory_space=pltpu.VMEM)
SMEM = pl.BlockSpec(memory_space=pltpu.SMEM)
ANY = pl.BlockSpec(memory_space=pl.ANY)
HBM = pl.BlockSpec(memory_space=pltpu.HBM)
NT = (((1,), (1,)), ((), ()))
MIB = 1 << 20


def iota(shape, dim):
    return lax.broadcasted_iota(I32, shape, dim)


def params(mib):
    return pltpu.CompilerParams(vmem_limit_bytes=mib * MIB)


def cost(flops, nbytes):
    return pl.CostEstimate(flops=int(flops), bytes_accessed=int(nbytes), transcendentals=0)


def block_rows(features):
    full, rest = divmod(features, LANES)
    assert rest in (0, HALF)
    rows = full * BLOCK + (BLOCK // 2 if rest else 0)
    return full, rest, rows


def pool_kernel(counts, seq, slot, win, enc, out):
    samples, cap = win.shape
    features, tokens = enc.shape
    groups = out.shape[0]
    full, rest, rows = block_rows(features)
    ids = win[...]
    pair = jnp.concatenate([ids, ids], axis=1)
    tiled = jnp.concatenate([pair] * (tokens // (2 * cap)), axis=1)
    lane = iota((samples, tokens), 1)
    mine = (lane // cap) == iota((samples, tokens), 0)
    ids_row = jnp.sum(jnp.where(mine, tiled, 0), axis=0, keepdims=True)
    lane = iota((1, tokens), 1)
    owner, place = lane // cap, lane % cap
    live = jnp.zeros((1, tokens), I32)
    base = jnp.zeros((1, tokens), I32)
    note = jnp.zeros((groups, NOTE, LANES), I32)
    target = iota((groups, NOTE, LANES), 0)
    for n in range(samples):
        live = jnp.where(owner == n, counts[n], live)
        base = jnp.where(owner == n, seq[n] * BLOCK, base)
        note = jnp.where(target == seq[n], slot[n] + 1, note)
    key = jnp.where(place < live, base + ids_row, -1)
    out[:, rows:, :] = note.astype(F32).astype(BF16)
    ones = jnp.ones((tokens, LANES), BF16)
    per = min(groups, 16)
    for g in range(0, groups, per):
        hot = (iota((per * BLOCK, tokens), 0) + g * BLOCK == key).astype(F32).astype(BF16)
        number = jnp.dot(hot, ones, preferred_element_type=F32)
        scale = 1.0 / jnp.maximum(number, 1.0)
        for j in range(full):
            part = enc[j * LANES : (j + 1) * LANES, :]
            got = lax.dot_general(hot, part, NT, preferred_element_type=F32) * scale
            got = got.astype(BF16).reshape(per, BLOCK, LANES)
            out[g : g + per, j * BLOCK : (j + 1) * BLOCK, :] = got
        if rest:
            part = enc[full * LANES :, :]
            part = jnp.concatenate([part, part], axis=0)
            got = lax.dot_general(hot, part, NT, preferred_element_type=F32) * scale
            got = got.reshape(per, BLOCK, LANES)
            low, high = got[:, : BLOCK // 2], got[:, BLOCK // 2 :]
            left = iota(low.shape, 2) < HALF
            out[g : g + per, full * BLOCK : rows, :] = jnp.where(left, low, high).astype(BF16)


def place_kernel(came, out):
    groups = came.shape[0]
    total, features = out.shape
    full, rest, rows = block_rows(features)
    note = came[:, rows : rows + NOTE, :].astype(F32)[:, 0, :].astype(BF16)
    spread = (iota((groups, groups * BLOCK), 1) // BLOCK == iota((groups, groups * BLOCK), 0)).astype(F32).astype(BF16)
    tn = (((0,), (0,)), ((), ()))
    slot_row = lax.dot_general(note, spread, tn, preferred_element_type=F32)[:1, :]
    lane = iota((1, groups * BLOCK), 1)
    key = (slot_row.astype(I32) - 1) * BLOCK + lane % BLOCK
    hot = (iota((total, groups * BLOCK), 0) == key).astype(F32).astype(BF16)
    for j in range(full):
        part = came[:, j * BLOCK : (j + 1) * BLOCK, :].reshape(groups * BLOCK, LANES)
        got = jnp.dot(hot, part, preferred_element_type=F32)
        out[:, j * LANES : (j + 1) * LANES] = got.astype(BF16)
    if rest:
        part = came[:, full * BLOCK : rows, :]
        twice = jnp.concatenate([part, part], axis=1).reshape(groups * BLOCK, LANES)
        got = jnp.dot(hot, twice, preferred_element_type=F32)
        low = iota((total, LANES), 0) % BLOCK < BLOCK // 2
        got = jnp.where(low, got, pltpu.roll(got, HALF, 1))
        out[:, full * LANES :] = got[:, :HALF].astype(BF16)


def fetch_kernel(w1, w2, v1, v2, sems):
    copies = [
        pltpu.make_async_copy(w1, v1, sems.at[0]),
        pltpu.make_async_copy(w2, v2, sems.at[1]),
    ]
    for copy in copies:
        copy.start()
    for copy in copies:
        copy.wait()


def columns(width, most=768):
    step = max(d for d in range(LANES, most + 1, LANES) if width % d == 0)
    return [(c, step) for c in range(0, width, step)]


def first_kernel(own, w, out):
    depth = own.shape[1]
    start = pl.multiple_of(lax.axis_index("tensor") * depth, NOTE)
    for c, n in columns(out.shape[1]):
        out[:, c : c + n] = jnp.dot(own[...], w[pl.ds(start, depth), c : c + n], preferred_element_type=F32)


def hidden_kernel(acc, other, w, b, w2, hidden, part):
    depth = other.shape[1]
    me = lax.axis_index("tensor")
    start = pl.multiple_of((1 - me) * depth, NOTE)
    for c, n in columns(acc.shape[1]):
        got = jnp.dot(other[...], w[pl.ds(start, depth), c : c + n], preferred_element_type=F32)
        got = got + acc[:, c : c + n] + b[:, c : c + n]
        hidden[:, c : c + n] = jax.nn.gelu(got, approximate=True).astype(BF16)
    width = part.shape[1]
    for c, n in columns(width, 384):
        col = pl.multiple_of((1 - me) * width + c, LANES)
        part[:, c : c + n] = jnp.dot(hidden[...], w2[:, pl.ds(col, n)], preferred_element_type=F32).astype(BF16)


def second_kernel(hidden, w2, part):
    width = part.shape[1]
    me = lax.axis_index("tensor")
    for c, n in columns(width, 384):
        col = pl.multiple_of(me * width + c, LANES)
        part[:, c : c + n] = jnp.dot(hidden[...], w2[:, pl.ds(col, n)], preferred_element_type=F32).astype(BF16)


def shards(encoded, counts, win_ids, dest_seq, dest_slot, w_first, b_first, w_second, b_second):
    groups = lax.axis_size("dp")
    samples = counts.shape[0]
    tokens, features = encoded.shape
    hidden_units = w_first.shape[1]
    width = b_second.shape[0]
    rows = block_rows(features)[2] + NOTE
    total = samples * BLOCK
    swap = ((0, 1), (1, 0))

    outgoing = pl.pallas_call(
        pool_kernel,
        out_shape=jax.ShapeDtypeStruct((groups, rows, LANES), BF16),
        in_specs=[SMEM, SMEM, SMEM, VMEM, VMEM],
        out_specs=VMEM,
        compiler_params=params(20),
        cost_estimate=cost(2e10, 6e7),
        name="pool",
    )(counts, dest_seq, dest_slot, win_ids, encoded.T)
    came = lax.all_to_all(outgoing, "dp", split_axis=0, concat_axis=0, tiled=True)
    w1, w2 = w_first, w_second
    own = pl.pallas_call(
        place_kernel,
        out_shape=jax.ShapeDtypeStruct((total, features), BF16),
        in_specs=[VMEM],
        out_specs=VMEM,
        compiler_params=params(20),
        cost_estimate=cost(2 * total * groups * BLOCK * features, 4 * total * features),
        name="place",
    )(came)
    other = lax.ppermute(own, "tensor", swap)
    acc = pl.pallas_call(
        first_kernel,
        out_shape=jax.ShapeDtypeStruct((total, hidden_units), F32),
        in_specs=[VMEM, VMEM],
        out_specs=VMEM,
        compiler_params=params(20),
        cost_estimate=cost(2 * total * features * hidden_units, 4 * total * hidden_units),
        name="first",
    )(own, w1)
    hidden, away = pl.pallas_call(
        hidden_kernel,
        out_shape=(
            jax.ShapeDtypeStruct((total, hidden_units), BF16),
            jax.ShapeDtypeStruct((total, width), BF16),
        ),
        in_specs=[VMEM] * 5,
        out_specs=(VMEM, VMEM),
        compiler_params=params(20),
        cost_estimate=cost(2 * total * (features + width) * hidden_units, 4 * total * hidden_units),
        name="hidden",
    )(acc, other, w1, b_first.reshape(1, -1), w2)
    back = lax.ppermute(away, "tensor", swap)
    kept = pl.pallas_call(
        second_kernel,
        out_shape=jax.ShapeDtypeStruct((total, width), BF16),
        in_specs=[VMEM, VMEM],
        out_specs=VMEM,
        compiler_params=params(20),
        cost_estimate=cost(2 * total * width * hidden_units, 4 * total * hidden_units),
        name="second",
    )(hidden, w2)
    return (kept.astype(F32) + back.astype(F32) + b_second).astype(BF16)


def solution(mesh):
    placed = (
        P("dp", "tensor"),
        P("dp"),
        P("dp", None),
        P("dp"),
        P("dp"),
        P(None, "tensor"),
        P("tensor"),
        P("tensor", None),
        P("tensor"),
    )
    return jax.shard_map(
        shards, mesh=mesh, in_specs=placed, out_specs=P("dp", "tensor"), check_vma=False
    )
```

time: 76.7 us -> 41.2 us (0.54)
  waiting for transfers between devices: 27.2 us -> 0.46 us
  blocking collectives: 2.23 us -> 26.5 us
  between operations: 13.5 us -> 0.11 us
  starting transfers between devices: 12.1 us -> 0.23 us
  matrix products: 11.6 us -> 0 us
  Pallas kernels: 0 us -> 8.57 us
  other arithmetic: 3.59 us -> 1.01 us
  local copies, waits for them, and re-layouts: 6 us -> 4.12 us
    all_to_all x0 -> x1, blocking collectives: none -> 26.5 us  [shards(): lax.all_to_all(outgoing, 'dp', split_axis=0, concat_axis=0, tiled=True)]
    all_to_all x2 -> x0, waiting for transfers between devices: 19.7 us -> none  [the longest x1 16.4 us: shards(): lax.all_to_all(outgoing, 'dp', split_axis=0, concat_axis=0, tiled=True)]
    all_to_all x2 -> x0, starting transfers between devices: 12.1 us -> none  [the longest x1 8.34 us: shards(): lax.all_to_all(offset_plus.astype(jnp.bfloat16), 'dp', split_axis=0, conc...]
    dot_general x4 -> x0, matrix products: 11.6 us -> none  [the longest x1 10.6 us: shards(): jnp.dot(hidden, w_second, preferred_element_type=jnp.float32)]
    pallas_call x0 -> x5, Pallas kernels: none -> 8.57 us  [the longest x1 3.09 us: shards(): pl.pallas_call(hidden_kernel, out_shape=(jax.ShapeDtypeStruct((total, hid...]
    unnamed x2 -> x0, waiting for transfers between devices: 7.54 us -> none
    all_gather x1 -> x0, blocking collectives: 2.23 us -> none  [shards(): lax.all_gather(packed, 'tensor', axis=1, tiled=True)]
    convert_element_type x3 -> x0, local copies, waits for them, and re-layouts: 1.69 us -> none  [the longest x1 0.95 us: shards(): jnp.einsum('es,swf->ewf', picker, pooled, preferred_element_type=jnp.floa...]
  transfers between devices with their start and end apart: 3 -> 2, of which waited for: 3 -> 1; matrix products, arithmetic and copies ran while one was open for 6% -> 0% of each run, Pallas kernels for 0% -> 8%
where the time goes in v1:
time: 41.2 us; the launch traced here: 41 us
  blocking collectives  26.5 us (64%)
  Pallas kernels  8.57 us (21%)
  local copies, waits for them, and re-layouts  4.12 us (10%)
  other arithmetic  1.01 us (2%)
  waiting for transfers between devices  0.46 us (1%)
    all_to_all x1, blocking collectives, shards(): lax.all_to_all(outgoing, 'dp', split_axis=0, concat_axis=0, tiled=True)  26.5 us
    unnamed x20, local copies, waits for them, and re-layouts  4.11 us
    pallas_call x1, Pallas kernels, shards(): pl.pallas_call(hidden_kernel, out_shape=(jax.ShapeDtypeStruct((total, hid...  3.09 us
    pallas_call x1, Pallas kernels, shards(): pl.pallas_call(second_kernel, out_shape=jax.ShapeDtypeStruct((total, widt...  2.02 us
    pallas_call x1, Pallas kernels, shards(): pl.pallas_call(pool_kernel, out_shape=jax.ShapeDtypeStruct((groups, rows,...  1.64 us
    pallas_call x1, Pallas kernels, shards(): pl.pallas_call(first_kernel, out_shape=jax.ShapeDtypeStruct((total, hidde...  1.09 us
    convert_element_type x1, other arithmetic, shards(): return (kept.astype(F32) + back.astype(F32) + b_second).astype(BF16)  1.01 us
  transfers between devices with their start and end apart: 2, of which 1 were waited for; matrix products, arithmetic and copies ran while one was open for 0% of the time, Pallas kernels for 8%

profile of v1, /device:TPU:0, one launch (start us, length us, event | category | flops | bytes accessed | tf_op | source)
XLA Modules:
  0.0 41.0 jit_solution(16643686589590087757)
XLA Ops:
  0.0 0.0 slice-start
  0.0 0.0 copy-start.1
  0.0 1.2 %copy-done.1 = bf16[512,576]{0,1:T(8,128)(2,1)S(1)} copy-done((bf16[512,576]{0,1:T(8,128)(2,1)S(1)}, bf16[512,576]{0,1:T(8,128)(2,1)}, u32[]{:S(2)}) %copy-start.1) | copy-done | bytes 589848
  1.2 0.0 copy-start.2
  1.2 0.9 %copy-done.2 = s32[8,64]{1,0:T(8,128)S(1)} copy-done((s32[8,64]{1,0:T(8,128)S(1)}, s32[8,64]{1,0:T(8,128)}, u32[]{:S(2)}) %copy-start.2) | copy-done | bytes 2072
  2.1 0.0 copy-start.3
  2.1 0.7 %copy-done.3 = s32[8]{0:T(128)S(1)} copy-done((s32[8]{0:T(128)S(1)}, s32[8]{0:T(128)}, u32[]{:S(2)}) %copy-start.3) | copy-done | bytes 56
  2.8 0.0 copy-start.4
  2.8 0.7 %copy-done.4 = s32[8]{0:T(128)S(1)} copy-done((s32[8]{0:T(128)S(1)}, s32[8]{0:T(128)}, u32[]{:S(2)}) %copy-start.4) | copy-done | bytes 56
  3.4 0.0 copy-start.5
  3.4 0.7 %copy-done.5 = s32[8]{0:T(128)S(1)} copy-done((s32[8]{0:T(128)S(1)}, s32[8]{0:T(128)}, u32[]{:S(2)}) %copy-start.5) | copy-done | bytes 56
  4.1 0.0 slice-start.1
  4.1 0.0 copy-start
  4.1 1.6 %pool.1 = bf16[16,152,128]{2,1,0:T(8,128)(2,1)S(1)} custom-call(s32[8]{0:T(128)S(1)} %copy-done.3, s32[8]{0:T(128)S(1)} %copy-done.4, s32[8]{0:T(128)S(1)} %copy-done.5, s32[8,64]{1,0:T(8,128)S(1)} %copy-done.2, bf16[576,512]{1,0:T(8,128)(2,1)S(1)} %bitcast.3), custom_call_target="tpu_custom_call" | custom-call | flops 20000000000 | bytes 60000000 | tf_op jit(solution)/shard_map/pool/pallas_call | solution.py:165
  5.8 0.0 copy-start.6
  5.8 26.5 %all_to_all.5.came = bf16[16,152,128]{2,1,0:T(8,128)(2,1)S(1)} all-to-all(bf16[16,152,128]{2,1,0:T(8,128)(2,1)S(1)} %pool.1), channel_id=1, replica_groups=mesh['dp'=16,'tensor'=2] {'dp'}, dimensions={0} | all-to-all | bytes 1245184 | tf_op jit(solution)/shard_map/all_to_all | solution.py:174
  32.3 0.7 %place.1.own = bf16[256,576]{1,0:T(8,128)(2,1)S(1)} custom-call(bf16[16,152,128]{2,1,0:T(8,128)(2,1)S(1)} %all_to_all.5.came), custom_call_target="tpu_custom_call" | custom-call | flops 150994944 | bytes 589824 | tf_op jit(solution)/shard_map/place/pallas_call | solution.py:176
  33.0 0.1 collective-permute-start
  33.1 0.0 copy-done.6
  33.1 0.0 slice-done
  33.1 0.0 slice-done.1
  33.1 1.1 %first.1.acc = f32[256,2304]{1,0:T(8,128)S(1)} custom-call(bf16[256,576]{1,0:T(8,128)(2,1)S(1)} %place.1.own, bf16[1152,2304]{1,0:T(8,128)(2,1)S(1)} %bitcast.2), custom_call_target="tpu_custom_call" | custom-call | flops 679477248 | bytes 2359296 | tf_op jit(solution)/shard_map/first/pallas_call | solution.py:186
  34.2 0.5 %collective-permute-done.other = bf16[256,576]{1,0:T(8,128)(2,1)S(1)} collective-permute-done((bf16[256,576]{1,0:T(8,128)(2,1)S(1)}, bf16[256,576]{1,0:T(8,128)(2,1)S(1)}, u32[]{:S(2)}, u32[]{:S(2)}) %collective-permute-start) | collective-permute-done | bytes 294944 | tf_op jit(solution)/shard_map/ppermute | solution.py:185
  34.7 0.0 copy-done
  34.7 3.1 %hidden.1 = (bf16[256,2304]{1,0:T(8,128)(2,1)S(1)}, bf16[256,1152]{1,0:T(8,128)(2,1)S(1)}) custom-call(f32[256,2304]{1,0:T(8,128)S(1)} %first.1.acc, bf16[256,576]{1,0:T(8,128)(2,1)S(1)} %collective-permute-done.other, bf16[1152,2304]{1,0:T(8,128)(2,1)S(1)} %bitcast.2, f32[1,2304]{1,0:T(1,128)S(1)} %reshape.4.b, bf16[2304,2304]{1,0:T(8,128)(2,1)S(1)} %copy-done), custom_call_target="tpu_custom_call" | custom-call | flops 2038431744 | bytes 2359296 | tf_op jit(solution)/shard_map/hidden/pallas_call | solution.py:195
  37.8 0.2 collective-permute-start.1
  37.9 0.0 copy-start.7
  37.9 2.0 %second.1 = bf16[256,1152]{1,0:T(8,128)(2,1)S(1)} custom-call(bf16[256,2304]{1,0:T(8,128)(2,1)S(1)} %get-tuple-element.7.hidden, bf16[2304,2304]{1,0:T(8,128)(2,1)S(1)} %copy-done), custom_call_target="tpu_custom_call" | custom-call | flops 1358954496 | bytes 2359296 | tf_op jit(solution)/shard_map/second/pallas_call | solution.py:208
  40.0 0.0 collective-permute-done.1
  40.0 0.0 copy-done.7
  40.0 1.0 %add_convert_fusion = bf16[256,1152]{1,0:T(8,128)(2,1)} fusion(bf16[256,1152]{1,0:T(8,128)(2,1)S(1)} %collective-permute-done.1, bf16[256,1152]{1,0:T(8,128)(2,1)S(1)} %second.1, f32[1152]{0:T(1024)S(1)} %copy-done.7), kind=kLoop, calls=%fused_computation | loop fusion | flops 1474560 | bytes 1774080 | tf_op jit(solution)/shard_map/convert_element_type | solution.py:217
  (2 shorter events, 0.0 us)
Async XLA Ops:
  0.0 33.1 %slice-start = ((s8[5308416]{0:T(1024)(128)(4,1)}), s8[4194304]{0:T(1024)(128)(4,1)S(1)}, s32[]{:S(2)}) async-start(s8[5308416]{0:T(1024)(128)(4,1)} %bitcast.1), calls=%async_computation.1 | async-start | bytes 8388608
  0.0 1.2 %copy-start.1 = (bf16[512,576]{0,1:T(8,128)(2,1)S(1)}, bf16[512,576]{0,1:T(8,128)(2,1)}, u32[]{:S(2)}) copy-start(bf16[512,576]{0,1:T(8,128)(2,1)} %param.9) | copy-start | bytes 1769476
  1.2 0.9 %copy-start.2 = (s32[8,64]{1,0:T(8,128)S(1)}, s32[8,64]{1,0:T(8,128)}, u32[]{:S(2)}) copy-start(s32[8,64]{1,0:T(8,128)} %win.1) | copy-start | bytes 6148
  2.1 0.7 %copy-start.3 = (s32[8]{0:T(128)S(1)}, s32[8]{0:T(128)}, u32[]{:S(2)}) copy-start(s32[8]{0:T(128)} %counts.1) | copy-start | bytes 100
  2.8 0.7 %copy-start.4 = (s32[8]{0:T(128)S(1)}, s32[8]{0:T(128)}, u32[]{:S(2)}) copy-start(s32[8]{0:T(128)} %seq.1) | copy-start | bytes 100
  3.4 0.7 %copy-start.5 = (s32[8]{0:T(128)S(1)}, s32[8]{0:T(128)}, u32[]{:S(2)}) copy-start(s32[8]{0:T(128)} %slot.1) | copy-start | bytes 100
  4.1 29.0 %slice-start.1 = ((s8[5308416]{0:T(1024)(128)(4,1)}), s8[1114112]{0:T(1024)(128)(4,1)S(1)}, s32[]{:S(2)}) async-start(s8[5308416]{0:T(1024)(128)(4,1)} %bitcast.1), calls=%async_computation.2 | async-start | bytes 2228224
  4.1 30.6 %copy-start = (bf16[2304,2304]{1,0:T(8,128)(2,1)S(1)}, bf16[2304,2304]{1,0:T(8,128)(2,1)}, u32[]{:S(2)}) copy-start(bf16[2304,2304]{1,0:T(8,128)(2,1)} %w2.3) | copy-start | bytes 31850500
  5.8 27.3 %copy-start.6 = (f32[2304]{0:T(1024)S(1)}, f32[2304]{0:T(1024)}, u32[]{:S(2)}) copy-start(f32[2304]{0:T(1024)} %param.15) | copy-start | bytes 27652
  33.0 1.7 %collective-permute-start = (bf16[256,576]{1,0:T(8,128)(2,1)S(1)}, bf16[256,576]{1,0:T(8,128)(2,1)S(1)}, u32[]{:S(2)}, u32[]{:S(2)}) collective-permute-start(bf16[256,576]{1,0:T(8,128)(2,1)S(1)} %place.1.own), channel_id=1, source_target_pairs={{0,1},{1,0},{2,3},{3,2},{4,5},{5,4},{6,7},{7,6},{8,9},{9,8},{10,11... | collective-permute-start | bytes 884744 | tf_op jit(solution)/shard_map/ppermute | solution.py:185
  37.8 2.2 %collective-permute-start.1 = (bf16[256,1152]{1,0:T(8,128)(2,1)S(1)}, bf16[256,1152]{1,0:T(8,128)(2,1)S(1)}, u32[]{:S(2)}, u32[]{:S(2)}) collective-permute-start(bf16[256,1152]{1,0:T(8,128)(2,1)S(1)} %get-tuple-element.8), channel_id=1, source_target_pairs={{0,1},{1,0},{2,3},{3,2},{4,5},{5,4},{6,7},{7,6},{8,9},{9,8},{10,11... | collective-permute-start | bytes 1769480 | tf_op jit(solution)/shard_map/ppermute | solution.py:207
  37.9 2.0 %copy-start.7 = (f32[1152]{0:T(1024)S(1)}, f32[1152]{0:T(1024)}, u32[]{:S(2)}) copy-start(f32[1152]{0:T(1024)} %param.17) | copy-start | bytes 13828

commit v2 on v1

v2 whole, which is shorter than its diff:
```python
import math

import jax
import jax.numpy as jnp
from jax import lax
from jax.experimental import pallas as pl
from jax.experimental.pallas import tpu as pltpu
from jax.sharding import PartitionSpec as P

BLOCK = 32
LANES = 128
HALF = LANES // 2
NOTE = 8
F32, BF16, I32 = jnp.float32, jnp.bfloat16, jnp.int32
VMEM = pl.BlockSpec(memory_space=pltpu.VMEM)
SMEM = pl.BlockSpec(memory_space=pltpu.SMEM)
ANY = pl.BlockSpec(memory_space=pl.ANY)
HBM = pl.BlockSpec(memory_space=pltpu.HBM)
NT = (((1,), (1,)), ((), ()))
TILE = 256
GRANT = 20 << 20
POOL_FLOPS, POOL_BYTES = 2e10, 6e7
GELU_A = (2 / math.pi) ** 0.5
GELU_B = 0.044715 * GELU_A


def iota(shape, dim):
    return lax.broadcasted_iota(I32, shape, dim)


def block_rows(features):
    full, rest = divmod(features, LANES)
    assert rest in (0, HALF)
    rows = full * BLOCK + (BLOCK // 2 if rest else 0)
    return full, rest, rows


def load_kernel(counts_in, seq_in, slot_in, win_in, enc_in, key, note, enc, counts, seq, slot, win, small, large):
    samples, cap = win.shape
    tokens = enc.shape[1]
    groups = note.shape[0]
    smalls = [
        pltpu.make_async_copy(a, b, small.at[i])
        for i, (a, b) in enumerate(((win_in, win), (counts_in, counts), (seq_in, seq), (slot_in, slot)))
    ]
    tall = pltpu.make_async_copy(enc_in, enc, large)
    for copy in smalls:
        copy.start()
    tall.start()
    for copy in smalls:
        copy.wait()
    ids = win[...]
    pair = jnp.concatenate([ids, ids], axis=1)
    tiled = jnp.concatenate([pair] * (tokens // (2 * cap)), axis=1)
    lane = iota((samples, tokens), 1)
    mine = (lane // cap) == iota((samples, tokens), 0)
    ids_row = jnp.sum(jnp.where(mine, tiled, 0), axis=0, keepdims=True)
    lane = iota((1, tokens), 1)
    owner, place = lane // cap, lane % cap
    live = jnp.zeros((1, tokens), I32)
    base = jnp.zeros((1, tokens), I32)
    notes = jnp.zeros((groups, NOTE, LANES), I32)
    target = iota((groups, NOTE, LANES), 0)
    for n in range(samples):
        live = jnp.where(owner == n, counts[n], live)
        base = jnp.where(owner == n, seq[n] * BLOCK, base)
        notes = jnp.where(target == seq[n], slot[n] + 1, notes)
    key[...] = jnp.where(place < live, base + ids_row, -1)
    note[...] = notes.astype(F32).astype(BF16)
    tall.wait()


def pool_kernel(key, note, enc, out):
    features, tokens = enc.shape
    groups = out.shape[0]
    full, rest, rows = block_rows(features)
    out[:, rows:, :] = note[...]
    ones = jnp.ones((tokens, LANES), BF16)
    per = min(groups, 16)
    for g in range(0, groups, per):
        hot = (iota((per * BLOCK, tokens), 0) + g * BLOCK == key[...]).astype(F32).astype(BF16)
        number = jnp.dot(hot, ones, preferred_element_type=F32)
        scale = 1.0 / jnp.maximum(number, 1.0)
        for j in range(full):
            part = enc[j * LANES : (j + 1) * LANES, :]
            got = lax.dot_general(hot, part, NT, preferred_element_type=F32) * scale
            got = got.astype(BF16).reshape(per, BLOCK, LANES)
            out[g : g + per, j * BLOCK : (j + 1) * BLOCK, :] = got
        if rest:
            part = enc[full * LANES :, :]
            part = jnp.concatenate([part, part], axis=0)
            got = lax.dot_general(hot, part, NT, preferred_element_type=F32) * scale
            got = got.reshape(per, BLOCK, LANES)
            low, high = got[:, : BLOCK // 2], got[:, BLOCK // 2 :]
            left = iota(low.shape, 2) < HALF
            out[g : g + per, full * BLOCK : rows, :] = jnp.where(left, low, high).astype(BF16)


def place_kernel(came, out):
    groups = came.shape[0]
    total, padded = out.shape
    rows = came.shape[1] - NOTE
    full = rows // BLOCK
    each = LANES // BLOCK
    turn = iota((NOTE, LANES), 1) // BLOCK
    keys = []
    for d in range(0, groups, each):
        key = came[d, rows:, :].astype(F32)
        for i in range(1, each):
            key = jnp.where(turn == i, came[d + i, rows:, :].astype(F32), key)
        keys.append(key)
    key = jnp.concatenate(keys, axis=1)[:1].astype(I32)
    key = (key - 1) * BLOCK + iota((1, groups * BLOCK), 1) % BLOCK
    hot = (iota((total, groups * BLOCK), 0) == key).astype(F32).astype(BF16)
    for j in range(full):
        part = came[:, j * BLOCK : (j + 1) * BLOCK, :].reshape(groups * BLOCK, LANES)
        got = jnp.dot(hot, part, preferred_element_type=F32)
        out[:, j * LANES : (j + 1) * LANES] = got.astype(BF16)
    if rows > full * BLOCK:
        part = came[:, full * BLOCK : rows, :]
        twice = jnp.concatenate([part, part], axis=1).reshape(groups * BLOCK, LANES)
        got = jnp.dot(hot, twice, preferred_element_type=F32)
        low = iota((total, LANES), 0) % BLOCK < BLOCK // 2
        left = iota((total, LANES), 1) < HALF
        out[:, full * LANES :] = jnp.where(low == left, got, pltpu.roll(got, HALF, 1)).astype(BF16)


def columns(width, most):
    step = max(d for d in range(LANES, most + 1, LANES) if width % d == 0)
    return [(c, step) for c in range(0, width, step)]


def first_kernel(own, w, out):
    depth = w.shape[0] // 2
    deep = depth // LANES * LANES
    start = pl.multiple_of(lax.axis_index("tensor") * depth, HALF)
    for c, n in columns(out.shape[1], 768):
        out[:, c : c + n] = jnp.dot(own[:, :deep], w[pl.ds(start, deep), c : c + n], preferred_element_type=F32)


def gelu(x):
    inner = x * (GELU_A + GELU_B * (x * x))
    half = 0.5 * x
    return half + half * jnp.tanh(inner)


def hidden_kernel(acc, own, other, w, b, w2, hidden, away, extra):
    me = lax.axis_index("tensor")
    depth = w.shape[0] // 2
    deep = depth // LANES * LANES
    mine = pl.multiple_of(me * depth, HALF)
    theirs = pl.multiple_of((1 - me) * depth, HALF)
    left = other[:, :deep]
    if deep < depth:
        low = iota((other.shape[0], LANES), 1) < HALF
        both = jnp.where(low, own[:, deep:].astype(F32), other[:, deep:].astype(F32)).astype(BF16)
        left = jnp.concatenate([left, both], axis=1)
    for c, n in columns(acc.shape[1], 768):
        right = w[pl.ds(theirs, deep), c : c + n]
        if deep < depth:
            right = jnp.concatenate(
                [right, w[pl.ds(mine + deep, HALF), c : c + n], w[pl.ds(theirs + deep, HALF), c : c + n]], axis=0
            )
        got = jnp.dot(left, right, preferred_element_type=F32)
        got = got + acc[:, c : c + n] + b[:, c : c + n]
        hidden[:, c : c + n] = gelu(got).astype(BF16)
    width = away.shape[1]
    odd = width % TILE
    window = width + odd
    base = (1 - me) * (width - odd)
    ends = []
    for c in range(0, window, TILE):
        col = pl.multiple_of(base + c, LANES)
        got = jnp.dot(hidden[...], w2[:, pl.ds(col, TILE)], preferred_element_type=F32).astype(BF16)
        for h in range(0, TILE, LANES):
            piece = got[:, h : h + LANES]
            if odd and (c + h == 0 or c + h == window - LANES):
                ends.append(piece.astype(F32))
            else:
                at = c + h - LANES * (1 - me) if odd else c + h
                away[:, pl.ds(pl.multiple_of(at, LANES), LANES)] = piece
    if odd:
        at = pl.multiple_of((1 - me) * (width - LANES), LANES)
        away[:, pl.ds(at, LANES)] = jnp.where(me == 0, ends[1], ends[0]).astype(BF16)
        extra[...] = jnp.where(me == 0, ends[0], ends[1]).astype(BF16)


def second_kernel(hidden, w2, part):
    width = w2.shape[1] // 2
    base = lax.axis_index("tensor") * (width + width % TILE)
    for c in range(0, part.shape[1], TILE):
        col = pl.multiple_of(base + c, LANES)
        part[:, c : c + TILE] = jnp.dot(hidden[...], w2[:, pl.ds(col, TILE)], preferred_element_type=F32).astype(BF16)


def final_kernel(part, extra, back, b, out, held, sems):
    me = lax.axis_index("tensor")
    width = out.shape[1]
    odd = width % TILE
    done = part.shape[1]
    copies = []

    def put(at, size, value):
        at = pl.multiple_of(at, LANES)
        total = value + back[:, pl.ds(at, size)].astype(F32) + b[:, pl.ds(at, size)]
        held[:, pl.ds(at, size)] = total.astype(BF16)
        copies.append(
            pltpu.make_async_copy(held.at[:, pl.ds(at, size)], out.at[:, pl.ds(at, size)], sems.at[len(copies)])
        )
        copies[-1].start()

    for c in range(0, done, TILE):
        put(me * odd + c, TILE, part[:, c : c + TILE].astype(F32))
    if odd:
        put((1 - me) * (width - odd), odd, extra[...].astype(F32))
    for copy in copies:
        copy.wait()


def in_hbm(x):
    return pltpu.with_memory_space_constraint(x, pltpu.HBM)


def call(kernel, shapes, specs, out_specs, flops, nbytes, scratch=()):
    return pl.pallas_call(
        kernel,
        out_shape=shapes,
        in_specs=specs,
        out_specs=out_specs,
        scratch_shapes=list(scratch),
        compiler_params=pltpu.CompilerParams(vmem_limit_bytes=GRANT),
        cost_estimate=pl.CostEstimate(flops=int(flops), bytes_accessed=int(nbytes), transcendentals=0),
        name=kernel.__name__.removesuffix("_kernel"),
    )


def shards(encoded, counts, win_ids, dest_seq, dest_slot, w_first, b_first, w_second, b_second):
    groups = lax.axis_size("dp")
    samples = counts.shape[0]
    tokens, features = encoded.shape
    units = w_first.shape[1]
    width = b_second.shape[0]
    full, rest, rows = block_rows(features)
    total = samples * BLOCK
    swap = ((0, 1), (1, 0))
    shape = jax.ShapeDtypeStruct
    dma = pltpu.SemaphoreType.DMA
    ints = pltpu.SMEM((samples,), I32)
    odd = width % TILE
    early = width - odd

    key, note, enc = call(
        load_kernel,
        (pltpu.VMEM((1, tokens), I32), pltpu.VMEM((groups, NOTE, LANES), BF16), pltpu.VMEM((features, tokens), BF16)),
        [HBM] * 5,
        (VMEM, VMEM, VMEM),
        0,
        2 * tokens * features,
        [ints, ints, ints, pltpu.VMEM(win_ids.shape, I32), dma((4,)), dma],
    )(in_hbm(counts), in_hbm(dest_seq), in_hbm(dest_slot), in_hbm(win_ids), in_hbm(encoded.T))
    outgoing = call(
        pool_kernel,
        shape((groups, rows + NOTE, LANES), BF16),
        [VMEM] * 3,
        VMEM,
        POOL_FLOPS,
        POOL_BYTES,
    )(key, note, enc)
    came = lax.all_to_all(outgoing, "dp", split_axis=0, concat_axis=0, tiled=True)
    own = call(
        place_kernel,
        shape((total, (full + (rest > 0)) * LANES), BF16),
        [VMEM],
        VMEM,
        2 * total * groups * BLOCK * features,
        4 * total * features,
    )(came)
    other = lax.ppermute(own, "tensor", swap)
    acc = call(
        first_kernel,
        shape((total, units), F32),
        [VMEM] * 2,
        VMEM,
        2 * total * features * units,
        4 * total * units,
    )(own, w_first)
    hidden, away, extra = call(
        hidden_kernel,
        (shape((total, units), BF16), shape((total, width), BF16), shape((total, LANES), BF16)),
        [VMEM] * 6,
        (VMEM, VMEM, VMEM),
        2 * total * (features + width) * units,
        4 * total * units,
    )(acc, own, other, w_first, b_first.reshape(1, -1), w_second)
    back = lax.ppermute(away, "tensor", swap)
    part = call(
        second_kernel,
        shape((total, early), BF16),
        [VMEM] * 2,
        VMEM,
        2 * total * early * units,
        4 * total * units,
    )(hidden, w_second)
    return call(
        final_kernel,
        shape((total, width), BF16),
        [VMEM] * 4,
        ANY,
        total * width,
        4 * total * width,
        [pltpu.VMEM((total, width), BF16), dma((early // TILE + 1,))],
    )(part, extra, back, b_second.reshape(1, -1))


def solution(mesh):
    placed = (
        P("dp", "tensor"),
        P("dp"),
        P("dp", None),
        P("dp"),
        P("dp"),
        P(None, "tensor"),
        P("tensor"),
        P("tensor", None),
        P("tensor"),
    )
    return jax.shard_map(
        shards, mesh=mesh, in_specs=placed, out_specs=P("dp", "tensor"), check_vma=False
    )
```

time: 41.2 us -> 37 us (0.90)
  local copies, waits for them, and re-layouts: 4.12 us -> 0.05 us
  other arithmetic: 1.01 us -> 0.01 us
  waiting for transfers between devices: 0.46 us -> 1.22 us
    unnamed x20 -> x12, local copies, waits for them, and re-layouts: 4.11 us -> 0.04 us
    convert_element_type x1 -> x0, other arithmetic: 1.01 us -> none  [shards(): return (kept.astype(F32) + back.astype(F32) + b_second).astype(BF16)]
    ppermute x1, waiting for transfers between devices: 0.01 us -> 0.44 us  [shards(): back = lax.ppermute(away, 'tensor', swap)]
    pallas_call x5 -> x7, Pallas kernels: 8.57 us -> 8.62 us  [the longest x1 2.85 us: shards(): call(hidden_kernel, (shape((total, units), BF16), shape((total, width), B...]
  transfers between devices with their start and end apart: 2 -> 2, of which waited for: 1 -> 2; matrix products, arithmetic and copies ran while one was open for 0% -> 0% of each run, Pallas kernels for 8% -> 6%
where the time goes in v2:
time: 37 us; the launch traced here: 36.8 us
  blocking collectives  26.5 us (72%)
  Pallas kernels  8.62 us (23%)
  waiting for transfers between devices  1.22 us (3%)
    all_to_all x1, blocking collectives, shards(): lax.all_to_all(outgoing, 'dp', split_axis=0, concat_axis=0, tiled=True)  26.5 us
    pallas_call x1, Pallas kernels, shards(): call(hidden_kernel, (shape((total, units), BF16), shape((total, width), B...  2.85 us
    pallas_call x1, Pallas kernels, shards(): call(second_kernel, shape((total, early), BF16), [VMEM] * 2, VMEM, 2 * to...  1.42 us
    pallas_call x1, Pallas kernels, shards(): call(load_kernel, (pltpu.VMEM((1, tokens), I32), pltpu.VMEM((groups, NOTE...  1.12 us
    pallas_call x1, Pallas kernels, shards(): call(pool_kernel, shape((groups, rows + NOTE, LANES), BF16), [VMEM] * 3,...  0.98 us
    pallas_call x1, Pallas kernels, shards(): call(final_kernel, shape((total, width), BF16), [VMEM] * 4, ANY, total *...  0.9 us
    pallas_call x1, Pallas kernels, shards(): call(first_kernel, shape((total, units), F32), [VMEM] * 2, VMEM, 2 * tota...  0.79 us
    ppermute x1, waiting for transfers between devices, shards(): other = lax.ppermute(own, 'tensor', swap)  0.77 us
  transfers between devices with their start and end apart: 2, of which 2 were waited for; matrix products, arithmetic and copies ran while one was open for 0% of the time, Pallas kernels for 6%

profile of v2, /device:TPU:0, one launch (start us, length us, event | category | flops | bytes accessed | tf_op | source)
XLA Modules:
  0.0 36.8 jit_solution(1033445058377728941)
XLA Ops:
  0.0 1.1 %load.1 = (s32[1,512]{1,0:T(1,128)S(1)}, bf16[16,8,128]{2,1,0:T(8,128)(2,1)S(1)}, bf16[576,512]{1,0:T(8,128)(2,1)S(1)}) custom-call(s32[8]{0:T(128)} %counts_in.1, s32[8]{0:T(128)} %seq_in.1, s32[8]{0:T(128)} %slot_in.1, s32[8,64]{1,0:T(8,128)} %win_in.1, bf16[576,512]{1,0:T(8,128)(2,1)} %bitcast.3), custom_call_target="tpu_custom_call" | custom-call | bytes 589824 | tf_op jit(solution)/shard_map/load/pallas_call | solution.py:252
  1.1 0.0 slice-start
  1.1 0.0 copy-start.1
  1.2 0.0 copy-start
  1.2 0.0 slice-start.1
  1.2 0.0 slice-start.2
  1.2 1.0 %pool.1 = bf16[16,152,128]{2,1,0:T(8,128)(2,1)S(1)} custom-call(s32[1,512]{1,0:T(1,128)S(1)} %get-tuple-element.11.key, bf16[16,8,128]{2,1,0:T(8,128)(2,1)S(1)} %get-tuple-element.12.note, bf16[576,512]{1,0:T(8,128)(2,1)S(1)} %get-tuple-element.13.enc), custom_call_target="tpu_custom_call" | custom-call | flops 20000000000 | bytes 60000000 | tf_op jit(solution)/shard_map/pool/pallas_call | solution.py:261
  2.2 26.5 %all_to_all.5.came = bf16[16,152,128]{2,1,0:T(8,128)(2,1)S(1)} all-to-all(bf16[16,152,128]{2,1,0:T(8,128)(2,1)S(1)} %pool.1), channel_id=1, replica_groups=mesh['dp'=16,'tensor'=2] {'dp'}, dimensions={0} | all-to-all | bytes 1245184 | tf_op jit(solution)/shard_map/all_to_all | solution.py:269
  28.7 0.6 %place.1.own = bf16[256,640]{1,0:T(8,128)(2,1)S(1)} custom-call(bf16[16,152,128]{2,1,0:T(8,128)(2,1)S(1)} %all_to_all.5.came), custom_call_target="tpu_custom_call" | custom-call | flops 150994944 | bytes 589824 | tf_op jit(solution)/shard_map/place/pallas_call | solution.py:270
  29.2 0.1 collective-permute-start
  29.3 0.0 copy-done.1
  29.4 0.0 copy-done
  29.4 0.8 %first.1.acc = f32[256,2304]{1,0:T(8,128)S(1)} custom-call(bf16[256,640]{1,0:T(8,128)(2,1)S(1)} %place.1.own, bf16[1152,2304]{1,0:T(8,128)(2,1)S(1)} %copy-done), custom_call_target="tpu_custom_call" | custom-call | flops 679477248 | bytes 2359296 | tf_op jit(solution)/shard_map/first/pallas_call | solution.py:279
  30.2 0.0 copy-start.2
  30.2 0.8 %collective-permute-done.other = bf16[256,640]{1,0:T(8,128)(2,1)S(1)} collective-permute-done((bf16[256,640]{1,0:T(8,128)(2,1)S(1)}, bf16[256,640]{1,0:T(8,128)(2,1)S(1)}, u32[]{:S(2)}, u32[]{:S(2)}) %collective-permute-start) | collective-permute-done | bytes 327712 | tf_op jit(solution)/shard_map/ppermute | solution.py:278
  30.9 0.0 slice-done
  30.9 0.0 slice-done.1
  30.9 0.0 slice-done.2
  31.0 2.9 %hidden.1 = (bf16[256,2304]{1,0:T(8,128)(2,1)S(1)}, bf16[256,1152]{1,0:T(8,128)(2,1)S(1)}, bf16[256,128]{1,0:T(8,128)(2,1)S(1)}) custom-call(f32[256,2304]{1,0:T(8,128)S(1)} %first.1.acc, bf16[256,640]{1,0:T(8,128)(2,1)S(1)} %place.1.own, bf16[256,640]{1,0:T(8,128)(2,1)S(1)} %collective-permute-done.other, bf16[1152,2304]{1,0:T(8,128)(2,1)S(1)} %copy-done, ...), custom_call_target="tpu_custom_call" | custom-call | flops 2038431744 | bytes 2359296 | tf_op jit(solution)/shard_map/hidden/pallas_call | solution.py:287
  33.8 0.2 collective-permute-start.1
  34.0 0.0 copy-done.2
  34.0 1.4 %second.1.part = bf16[256,1024]{1,0:T(8,128)(2,1)S(1)} custom-call(bf16[256,2304]{1,0:T(8,128)(2,1)S(1)} %get-tuple-element.14.hidden, bf16[2304,2304]{1,0:T(8,128)(2,1)S(1)} %bitcast.2), custom_call_target="tpu_custom_call" | custom-call | flops 1207959552 | bytes 2359296 | tf_op jit(solution)/shard_map/second/pallas_call | solution.py:296
  35.4 0.4 %collective-permute-done.1.back = bf16[256,1152]{1,0:T(8,128)(2,1)S(1)} collective-permute-done((bf16[256,1152]{1,0:T(8,128)(2,1)S(1)}, bf16[256,1152]{1,0:T(8,128)(2,1)S(1)}, u32[]{:S(2)}, u32[]{:S(2)}) %collective-permute-start.1) | collective-permute-done | bytes 589856 | tf_op jit(solution)/shard_map/ppermute | solution.py:295
  35.9 0.9 %final.1 = bf16[256,1152]{1,0:T(8,128)(2,1)} custom-call(bf16[256,1024]{1,0:T(8,128)(2,1)S(1)} %second.1.part, bf16[256,128]{1,0:T(8,128)(2,1)S(1)} %get-tuple-element.15.extra, bf16[256,1152]{1,0:T(8,128)(2,1)S(1)} %collective-permute-done.1.back, f32[1,1152]{1,0:T(1,128)S(1)} %reshape.7.b), custom_call_target="tpu_custom_call" | custom-call | flops 294912 | bytes 1179648 | tf_op jit(solution)/shard_map/final/pallas_call | solution.py:304
  (3 shorter events, 0.0 us)
Async XLA Ops:
  1.1 29.8 %slice-start = ((s8[10616832]{0:T(1024)(128)(4,1)}), s8[4194304]{0:T(1024)(128)(4,1)S(1)}, s32[]{:S(2)}) async-start(s8[10616832]{0:T(1024)(128)(4,1)} %bitcast.1), calls=%async_computation.1 | async-start | bytes 8388608
  1.1 28.2 %copy-start.1 = (f32[2304]{0:T(1024)S(1)}, f32[2304]{0:T(1024)}, u32[]{:S(2)}) copy-start(f32[2304]{0:T(1024)} %param.15) | copy-start | bytes 27652
  1.2 28.2 %copy-start = (bf16[1152,2304]{1,0:T(8,128)(2,1)S(1)}, bf16[1152,2304]{1,0:T(8,128)(2,1)}, u32[]{:S(2)}) copy-start(bf16[1152,2304]{1,0:T(8,128)(2,1)} %w.3) | copy-start | bytes 15925252
  1.2 29.8 %slice-start.1 = ((s8[10616832]{0:T(1024)(128)(4,1)}), s8[4194304]{0:T(1024)(128)(4,1)S(1)}, s32[]{:S(2)}) async-start(s8[10616832]{0:T(1024)(128)(4,1)} %bitcast.1), calls=%async_computation.2 | async-start | bytes 8388608
  1.2 29.8 %slice-start.2 = ((s8[10616832]{0:T(1024)(128)(4,1)}), s8[2228224]{0:T(1024)(128)(4,1)S(1)}, s32[]{:S(2)}) async-start(s8[10616832]{0:T(1024)(128)(4,1)} %bitcast.1), calls=%async_computation.3 | async-start | bytes 4456448
  29.2 1.7 %collective-permute-start = (bf16[256,640]{1,0:T(8,128)(2,1)S(1)}, bf16[256,640]{1,0:T(8,128)(2,1)S(1)}, u32[]{:S(2)}, u32[]{:S(2)}) collective-permute-start(bf16[256,640]{1,0:T(8,128)(2,1)S(1)} %place.1.own), channel_id=1, source_target_pairs={{0,1},{1,0},{2,3},{3,2},{4,5},{5,4},{6,7},{7,6},{8,9},{9,8},{10,11... | collective-permute-start | bytes 983048 | tf_op jit(solution)/shard_map/ppermute | solution.py:278
  30.2 3.9 %copy-start.2 = (f32[1152]{0:T(1024)S(1)}, f32[1152]{0:T(1024)}, u32[]{:S(2)}) copy-start(f32[1152]{0:T(1024)} %param.17) | copy-start | bytes 13828
  33.8 2.1 %collective-permute-start.1 = (bf16[256,1152]{1,0:T(8,128)(2,1)S(1)}, bf16[256,1152]{1,0:T(8,128)(2,1)S(1)}, u32[]{:S(2)}, u32[]{:S(2)}) collective-permute-start(bf16[256,1152]{1,0:T(8,128)(2,1)S(1)} %get-tuple-element.16), channel_id=1, source_target_pairs={{0,1},{1,0},{2,3},{3,2},{4,5},{5,4},{6,7},{7,6},{8,9},{9,8},{10,11... | collective-permute-start | bytes 1769480 | tf_op jit(solution)/shard_map/ppermute | solution.py:295

commit v3 on v2

--- a/solution.py
+++ b/solution.py
@@ -1,3 +1,4 @@
+import functools
 import math
 
 import jax
@@ -35,7 +36,7 @@
     return full, rest, rows
 
 
-def load_kernel(counts_in, seq_in, slot_in, win_in, enc_in, key, note, enc, counts, seq, slot, win, small, large):
+def load_kernel(shift, counts_in, seq_in, slot_in, win_in, enc_in, key, note, enc, counts, seq, slot, win, small, large):
     samples, cap = win.shape
     tokens = enc.shape[1]
     groups = note.shape[0]
@@ -62,9 +63,11 @@
     notes = jnp.zeros((groups, NOTE, LANES), I32)
     target = iota((groups, NOTE, LANES), 0)
     for n in range(samples):
+        goal = seq[n] + shift
+        goal = jnp.where(goal >= groups, goal - groups, goal)
         live = jnp.where(owner == n, counts[n], live)
-        base = jnp.where(owner == n, seq[n] * BLOCK, base)
-        notes = jnp.where(target == seq[n], slot[n] + 1, notes)
+        base = jnp.where(owner == n, goal * BLOCK, base)
+        notes = jnp.where(target == goal, slot[n] + 1, notes)
     key[...] = jnp.where(place < live, base + ids_row, -1)
     note[...] = notes.astype(F32).astype(BF16)
     tall.wait()
@@ -230,7 +233,7 @@
         scratch_shapes=list(scratch),
         compiler_params=pltpu.CompilerParams(vmem_limit_bytes=GRANT),
         cost_estimate=pl.CostEstimate(flops=int(flops), bytes_accessed=int(nbytes), transcendentals=0),
-        name=kernel.__name__.removesuffix("_kernel"),
+        name=getattr(kernel, "func", kernel).__name__.removesuffix("_kernel"),
     )
 
 
@@ -248,9 +251,11 @@
     ints = pltpu.SMEM((samples,), I32)
     odd = width % TILE
     early = width - odd
+    lead = groups * 3 // 4 - 1
+    ring = [[(lead + i) % groups for i in range(groups)]]
 
     key, note, enc = call(
-        load_kernel,
+        functools.partial(load_kernel, groups - lead),
         (pltpu.VMEM((1, tokens), I32), pltpu.VMEM((groups, NOTE, LANES), BF16), pltpu.VMEM((features, tokens), BF16)),
         [HBM] * 5,
         (VMEM, VMEM, VMEM),
@@ -266,7 +271,7 @@
         POOL_FLOPS,
         POOL_BYTES,
     )(key, note, enc)
-    came = lax.all_to_all(outgoing, "dp", split_axis=0, concat_axis=0, tiled=True)
+    came = lax.all_to_all(outgoing, "dp", split_axis=0, concat_axis=0, tiled=True, axis_index_groups=ring)
     own = call(
         place_kernel,
         shape((total, (full + (rest > 0)) * LANES), BF16),

time: 37 us -> 33.8 us (0.914)
  blocking collectives: 26.5 us -> 23.3 us
    all_to_all x1, blocking collectives: 26.5 us -> 23.3 us  [shards(): lax.all_to_all(outgoing, 'dp', split_axis=0, concat_axis=0, tiled=True, a...]
  transfers between devices with their start and end apart: 2 -> 2, of which waited for: 2 -> 2; matrix products, arithmetic and copies ran while one was open for 0% -> 0% of each run, Pallas kernels for 6% -> 7%
where the time goes in v3:
time: 33.8 us; the launch traced here: 33.6 us
  blocking collectives  23.3 us (69%)
  Pallas kernels  8.62 us (26%)
  waiting for transfers between devices  1.22 us (4%)
    all_to_all x1, blocking collectives, shards(): lax.all_to_all(outgoing, 'dp', split_axis=0, concat_axis=0, tiled=True, a...  23.3 us
    pallas_call x1, Pallas kernels, shards(): call(hidden_kernel, (shape((total, units), BF16), shape((total, width), B...  2.85 us
    pallas_call x1, Pallas kernels, shards(): call(second_kernel, shape((total, early), BF16), [VMEM] * 2, VMEM, 2 * to...  1.42 us
    pallas_call x1, Pallas kernels, shards(): call(functools.partial(load_kernel, groups - lead), (pltpu.VMEM((1, token...  1.12 us
    pallas_call x1, Pallas kernels, shards(): call(pool_kernel, shape((groups, rows + NOTE, LANES), BF16), [VMEM] * 3,...  0.98 us
    pallas_call x1, Pallas kernels, shards(): call(final_kernel, shape((total, width), BF16), [VMEM] * 4, ANY, total *...  0.9 us
    pallas_call x1, Pallas kernels, shards(): call(first_kernel, shape((total, units), F32), [VMEM] * 2, VMEM, 2 * tota...  0.79 us
    ppermute x1, waiting for transfers between devices, shards(): other = lax.ppermute(own, 'tensor', swap)  0.77 us
  transfers between devices with their start and end apart: 2, of which 2 were waited for; matrix products, arithmetic and copies ran while one was open for 0% of the time, Pallas kernels for 7%

profile of v3, /device:TPU:0, one launch (start us, length us, event | category | flops | bytes accessed | tf_op | source)
XLA Modules:
  0.0 33.6 jit_solution(3863799726866906671)
XLA Ops:
  0.0 1.1 %load.1 = (s32[1,512]{1,0:T(1,128)S(1)}, bf16[16,8,128]{2,1,0:T(8,128)(2,1)S(1)}, bf16[576,512]{1,0:T(8,128)(2,1)S(1)}) custom-call(s32[8]{0:T(128)} %counts_in.1, s32[8]{0:T(128)} %seq_in.1, s32[8]{0:T(128)} %slot_in.1, s32[8,64]{1,0:T(8,128)} %win_in.1, bf16[576,512]{1,0:T(8,128)(2,1)} %bitcast.3), custom_call_target="tpu_custom_call" | custom-call | bytes 589824 | tf_op jit(solution)/shard_map/load/pallas_call | solution.py:257
  1.1 0.0 slice-start
  1.1 0.0 copy-start.1
  1.2 0.0 copy-start
  1.2 0.0 slice-start.1
  1.2 0.0 slice-start.2
  1.2 1.0 %pool.1 = bf16[16,152,128]{2,1,0:T(8,128)(2,1)S(1)} custom-call(s32[1,512]{1,0:T(1,128)S(1)} %get-tuple-element.11.key, bf16[16,8,128]{2,1,0:T(8,128)(2,1)S(1)} %get-tuple-element.12.note, bf16[576,512]{1,0:T(8,128)(2,1)S(1)} %get-tuple-element.13.enc), custom_call_target="tpu_custom_call" | custom-call | flops 20000000000 | bytes 60000000 | tf_op jit(solution)/shard_map/pool/pallas_call | solution.py:266
  2.2 23.3 %all_to_all.5.came = bf16[16,152,128]{2,1,0:T(8,128)(2,1)S(1)} all-to-all(bf16[16,152,128]{2,1,0:T(8,128)(2,1)S(1)} %pool.1), channel_id=1, replica_groups={{22,24,26,28,30,0,2,4,6,8,10,12,14,16,18,20},{23,25,27,29,31,1,3,5,7,9,..., dimensions={0} | all-to-all | bytes 1245184 | tf_op jit(solution)/shard_map/all_to_all | solution.py:274
  25.5 0.6 %place.1.own = bf16[256,640]{1,0:T(8,128)(2,1)S(1)} custom-call(bf16[16,152,128]{2,1,0:T(8,128)(2,1)S(1)} %all_to_all.5.came), custom_call_target="tpu_custom_call" | custom-call | flops 150994944 | bytes 589824 | tf_op jit(solution)/shard_map/place/pallas_call | solution.py:275
  26.0 0.1 collective-permute-start
  26.1 0.0 copy-done.1
  26.1 0.0 copy-done
  26.1 0.8 %first.1.acc = f32[256,2304]{1,0:T(8,128)S(1)} custom-call(bf16[256,640]{1,0:T(8,128)(2,1)S(1)} %place.1.own, bf16[1152,2304]{1,0:T(8,128)(2,1)S(1)} %copy-done), custom_call_target="tpu_custom_call" | custom-call | flops 679477248 | bytes 2359296 | tf_op jit(solution)/shard_map/first/pallas_call | solution.py:284
  26.9 0.0 copy-start.2
  26.9 0.8 %collective-permute-done.other = bf16[256,640]{1,0:T(8,128)(2,1)S(1)} collective-permute-done((bf16[256,640]{1,0:T(8,128)(2,1)S(1)}, bf16[256,640]{1,0:T(8,128)(2,1)S(1)}, u32[]{:S(2)}, u32[]{:S(2)}) %collective-permute-start) | collective-permute-done | bytes 327712 | tf_op jit(solution)/shard_map/ppermute | solution.py:283
  27.7 0.0 slice-done
  27.7 0.0 slice-done.1
  27.7 0.0 slice-done.2
  27.7 2.9 %hidden.1 = (bf16[256,2304]{1,0:T(8,128)(2,1)S(1)}, bf16[256,1152]{1,0:T(8,128)(2,1)S(1)}, bf16[256,128]{1,0:T(8,128)(2,1)S(1)}) custom-call(f32[256,2304]{1,0:T(8,128)S(1)} %first.1.acc, bf16[256,640]{1,0:T(8,128)(2,1)S(1)} %place.1.own, bf16[256,640]{1,0:T(8,128)(2,1)S(1)} %collective-permute-done.other, bf16[1152,2304]{1,0:T(8,128)(2,1)S(1)} %copy-done, ...), custom_call_target="tpu_custom_call" | custom-call | flops 2038431744 | bytes 2359296 | tf_op jit(solution)/shard_map/hidden/pallas_call | solution.py:292
  30.6 0.2 collective-permute-start.1
  30.8 0.0 copy-done.2
  30.8 1.4 %second.1.part = bf16[256,1024]{1,0:T(8,128)(2,1)S(1)} custom-call(bf16[256,2304]{1,0:T(8,128)(2,1)S(1)} %get-tuple-element.14.hidden, bf16[2304,2304]{1,0:T(8,128)(2,1)S(1)} %bitcast.2), custom_call_target="tpu_custom_call" | custom-call | flops 1207959552 | bytes 2359296 | tf_op jit(solution)/shard_map/second/pallas_call | solution.py:301
  32.2 0.4 %collective-permute-done.1.back = bf16[256,1152]{1,0:T(8,128)(2,1)S(1)} collective-permute-done((bf16[256,1152]{1,0:T(8,128)(2,1)S(1)}, bf16[256,1152]{1,0:T(8,128)(2,1)S(1)}, u32[]{:S(2)}, u32[]{:S(2)}) %collective-permute-start.1) | collective-permute-done | bytes 589856 | tf_op jit(solution)/shard_map/ppermute | solution.py:300
  32.7 0.9 %final.1 = bf16[256,1152]{1,0:T(8,128)(2,1)} custom-call(bf16[256,1024]{1,0:T(8,128)(2,1)S(1)} %second.1.part, bf16[256,128]{1,0:T(8,128)(2,1)S(1)} %get-tuple-element.15.extra, bf16[256,1152]{1,0:T(8,128)(2,1)S(1)} %collective-permute-done.1.back, f32[1,1152]{1,0:T(1,128)S(1)} %reshape.7.b), custom_call_target="tpu_custom_call" | custom-call | flops 294912 | bytes 1179648 | tf_op jit(solution)/shard_map/final/pallas_call | solution.py:309
  (3 shorter events, 0.0 us)
Async XLA Ops:
  1.1 26.6 %slice-start = ((s8[10616832]{0:T(1024)(128)(4,1)}), s8[4194304]{0:T(1024)(128)(4,1)S(1)}, s32[]{:S(2)}) async-start(s8[10616832]{0:T(1024)(128)(4,1)} %bitcast.1), calls=%async_computation.1 | async-start | bytes 8388608
  1.1 25.0 %copy-start.1 = (f32[2304]{0:T(1024)S(1)}, f32[2304]{0:T(1024)}, u32[]{:S(2)}) copy-start(f32[2304]{0:T(1024)} %param.15) | copy-start | bytes 27652
  1.2 25.0 %copy-start = (bf16[1152,2304]{1,0:T(8,128)(2,1)S(1)}, bf16[1152,2304]{1,0:T(8,128)(2,1)}, u32[]{:S(2)}) copy-start(bf16[1152,2304]{1,0:T(8,128)(2,1)} %w.3) | copy-start | bytes 15925252
  1.2 26.6 %slice-start.1 = ((s8[10616832]{0:T(1024)(128)(4,1)}), s8[4194304]{0:T(1024)(128)(4,1)S(1)}, s32[]{:S(2)}) async-start(s8[10616832]{0:T(1024)(128)(4,1)} %bitcast.1), calls=%async_computation.2 | async-start | bytes 8388608
  1.2 26.6 %slice-start.2 = ((s8[10616832]{0:T(1024)(128)(4,1)}), s8[2228224]{0:T(1024)(128)(4,1)S(1)}, s32[]{:S(2)}) async-start(s8[10616832]{0:T(1024)(128)(4,1)} %bitcast.1), calls=%async_computation.3 | async-start | bytes 4456448
  26.0 1.7 %collective-permute-start = (bf16[256,640]{1,0:T(8,128)(2,1)S(1)}, bf16[256,640]{1,0:T(8,128)(2,1)S(1)}, u32[]{:S(2)}, u32[]{:S(2)}) collective-permute-start(bf16[256,640]{1,0:T(8,128)(2,1)S(1)} %place.1.own), channel_id=1, source_target_pairs={{0,1},{1,0},{2,3},{3,2},{4,5},{5,4},{6,7},{7,6},{8,9},{9,8},{10,11... | collective-permute-start | bytes 983048 | tf_op jit(solution)/shard_map/ppermute | solution.py:283
  26.9 3.9 %copy-start.2 = (f32[1152]{0:T(1024)S(1)}, f32[1152]{0:T(1024)}, u32[]{:S(2)}) copy-start(f32[1152]{0:T(1024)} %param.17) | copy-start | bytes 13828
  30.6 2.1 %collective-permute-start.1 = (bf16[256,1152]{1,0:T(8,128)(2,1)S(1)}, bf16[256,1152]{1,0:T(8,128)(2,1)S(1)}, u32[]{:S(2)}, u32[]{:S(2)}) collective-permute-start(bf16[256,1152]{1,0:T(8,128)(2,1)S(1)} %get-tuple-element.16), channel_id=1, source_target_pairs={{0,1},{1,0},{2,3},{3,2},{4,5},{5,4},{6,7},{7,6},{8,9},{9,8},{10,11... | collective-permute-start | bytes 1769480 | tf_op jit(solution)/shard_map/ppermute | solution.py:300

commit v4 on v3

--- a/solution.py
+++ b/solution.py
@@ -19,6 +19,7 @@
 HBM = pl.BlockSpec(memory_space=pltpu.HBM)
 NT = (((1,), (1,)), ((), ()))
 TILE = 256
+PIECES = 4
 GRANT = 20 << 20
 POOL_FLOPS, POOL_BYTES = 2e10, 6e7
 GELU_A = (2 / math.pi) ** 0.5
@@ -36,7 +37,7 @@
     return full, rest, rows
 
 
-def load_kernel(shift, counts_in, seq_in, slot_in, win_in, enc_in, key, note, enc, counts, seq, slot, win, small, large):
+def load_kernel(shift, counts_in, seq_in, slot_in, win_in, enc_in, hot, note, enc, counts, seq, slot, win, small, large):
     samples, cap = win.shape
     tokens = enc.shape[1]
     groups = note.shape[0]
@@ -68,35 +69,39 @@
         live = jnp.where(owner == n, counts[n], live)
         base = jnp.where(owner == n, goal * BLOCK, base)
         notes = jnp.where(target == goal, slot[n] + 1, notes)
-    key[...] = jnp.where(place < live, base + ids_row, -1)
+    key = jnp.where(place < live, base + ids_row, -1)
     note[...] = notes.astype(F32).astype(BF16)
+    rows = min(hot.shape[0], 2 * TILE)
+    for r in range(0, hot.shape[0], rows):
+        hot[r : r + rows, :] = (iota((rows, tokens), 0) + r == key).astype(F32).astype(BF16)
     tall.wait()
 
 
-def pool_kernel(key, note, enc, out):
+def pool_kernel(hot, note, enc, out):
     features, tokens = enc.shape
     groups = out.shape[0]
     full, rest, rows = block_rows(features)
     out[:, rows:, :] = note[...]
-    ones = jnp.ones((tokens, LANES), BF16)
+    ones = jnp.ones((LANES, tokens), BF16)
+    tail = enc[full * LANES :, :]
+    tail = jnp.concatenate([tail, tail, ones] if rest else [ones], axis=0)
     per = min(groups, 16)
     for g in range(0, groups, per):
-        hot = (iota((per * BLOCK, tokens), 0) + g * BLOCK == key[...]).astype(F32).astype(BF16)
-        number = jnp.dot(hot, ones, preferred_element_type=F32)
-        scale = 1.0 / jnp.maximum(number, 1.0)
-        for j in range(full):
-            part = enc[j * LANES : (j + 1) * LANES, :]
-            got = lax.dot_general(hot, part, NT, preferred_element_type=F32) * scale
-            got = got.astype(BF16).reshape(per, BLOCK, LANES)
-            out[g : g + per, j * BLOCK : (j + 1) * BLOCK, :] = got
+        pick = hot[g * BLOCK : (g + per) * BLOCK, :]
+        last = lax.dot_general(pick, tail, NT, preferred_element_type=F32)
+        scale = 1.0 / jnp.maximum(last[:, -LANES:], 1.0)
         if rest:
-            part = enc[full * LANES :, :]
-            part = jnp.concatenate([part, part], axis=0)
-            got = lax.dot_general(hot, part, NT, preferred_element_type=F32) * scale
-            got = got.reshape(per, BLOCK, LANES)
+            got = (last[:, :LANES] * scale).reshape(per, BLOCK, LANES)
             low, high = got[:, : BLOCK // 2], got[:, BLOCK // 2 :]
             left = iota(low.shape, 2) < HALF
             out[g : g + per, full * BLOCK : rows, :] = jnp.where(left, low, high).astype(BF16)
+        for c in range(0, full * LANES, TILE):
+            n = min(TILE, full * LANES - c)
+            both = lax.dot_general(pick, enc[c : c + n, :], NT, preferred_element_type=F32)
+            for j in range(0, n, LANES):
+                got = (both[:, j : j + LANES] * scale).astype(BF16).reshape(per, BLOCK, LANES)
+                at = (c + j) // LANES * BLOCK
+                out[g : g + per, at : at + BLOCK, :] = got
 
 
 def place_kernel(came, out):
@@ -115,10 +120,10 @@
     key = jnp.concatenate(keys, axis=1)[:1].astype(I32)
     key = (key - 1) * BLOCK + iota((1, groups * BLOCK), 1) % BLOCK
     hot = (iota((total, groups * BLOCK), 0) == key).astype(F32).astype(BF16)
-    for j in range(full):
-        part = came[:, j * BLOCK : (j + 1) * BLOCK, :].reshape(groups * BLOCK, LANES)
-        got = jnp.dot(hot, part, preferred_element_type=F32)
-        out[:, j * LANES : (j + 1) * LANES] = got.astype(BF16)
+    for j in range(0, full, 2):
+        parts = [came[:, i * BLOCK : (i + 1) * BLOCK, :].reshape(groups * BLOCK, LANES) for i in range(j, min(j + 2, full))]
+        got = jnp.dot(hot, jnp.concatenate(parts, axis=1), preferred_element_type=F32)
+        out[:, j * LANES : (j + len(parts)) * LANES] = got.astype(BF16)
     if rows > full * BLOCK:
         part = came[:, full * BLOCK : rows, :]
         twice = jnp.concatenate([part, part], axis=1).reshape(groups * BLOCK, LANES)
@@ -188,34 +193,27 @@
         extra[...] = jnp.where(me == 0, ends[0], ends[1]).astype(BF16)
 
 
-def second_kernel(hidden, w2, part):
-    width = w2.shape[1] // 2
-    base = lax.axis_index("tensor") * (width + width % TILE)
-    for c in range(0, part.shape[1], TILE):
-        col = pl.multiple_of(base + c, LANES)
-        part[:, c : c + TILE] = jnp.dot(hidden[...], w2[:, pl.ds(col, TILE)], preferred_element_type=F32).astype(BF16)
-
-
-def final_kernel(part, extra, back, b, out, held, sems):
+def second_kernel(hidden, w2, extra, part):
+    width = part.shape[1]
+    odd = width % TILE
     me = lax.axis_index("tensor")
-    width = out.shape[1]
-    odd = width % TILE
-    done = part.shape[1]
+    if odd:
+        part[:, pl.ds(pl.multiple_of((1 - me) * (width - odd), LANES), odd)] = extra[...]
+    for c in range(0, width - odd, TILE):
+        col = pl.multiple_of(me * (width + odd) + c, LANES)
+        got = jnp.dot(hidden[...], w2[:, pl.ds(col, TILE)], preferred_element_type=F32).astype(BF16)
+        part[:, pl.ds(pl.multiple_of(me * odd + c, LANES), TILE)] = got
+
+
+def final_kernel(part, back, b, out, held, sems):
+    pieces = sems.shape[0]
+    rows = out.shape[0] // pieces
     copies = []
-
-    def put(at, size, value):
-        at = pl.multiple_of(at, LANES)
-        total = value + back[:, pl.ds(at, size)].astype(F32) + b[:, pl.ds(at, size)]
-        held[:, pl.ds(at, size)] = total.astype(BF16)
-        copies.append(
-            pltpu.make_async_copy(held.at[:, pl.ds(at, size)], out.at[:, pl.ds(at, size)], sems.at[len(copies)])
-        )
+    for i in range(pieces):
+        at = slice(i * rows, (i + 1) * rows)
+        held[at, :] = (part[at, :].astype(F32) + back[at, :].astype(F32) + b[...]).astype(BF16)
+        copies.append(pltpu.make_async_copy(held.at[at], out.at[at], sems.at[i]))
         copies[-1].start()
-
-    for c in range(0, done, TILE):
-        put(me * odd + c, TILE, part[:, c : c + TILE].astype(F32))
-    if odd:
-        put((1 - me) * (width - odd), odd, extra[...].astype(F32))
     for copy in copies:
         copy.wait()
 
@@ -249,14 +247,12 @@
     shape = jax.ShapeDtypeStruct
     dma = pltpu.SemaphoreType.DMA
     ints = pltpu.SMEM((samples,), I32)
-    odd = width % TILE
-    early = width - odd
     lead = groups * 3 // 4 - 1
     ring = [[(lead + i) % groups for i in range(groups)]]
 
-    key, note, enc = call(
+    hot, note, enc = call(
         functools.partial(load_kernel, groups - lead),
-        (pltpu.VMEM((1, tokens), I32), pltpu.VMEM((groups, NOTE, LANES), BF16), pltpu.VMEM((features, tokens), BF16)),
+        (pltpu.VMEM((groups * BLOCK, tokens), BF16), pltpu.VMEM((groups, NOTE, LANES), BF16), pltpu.VMEM((features, tokens), BF16)),
         [HBM] * 5,
         (VMEM, VMEM, VMEM),
         0,
@@ -270,7 +266,7 @@
         VMEM,
         POOL_FLOPS,
         POOL_BYTES,
-    )(key, note, enc)
+    )(hot, note, enc)
     came = lax.all_to_all(outgoing, "dp", split_axis=0, concat_axis=0, tiled=True, axis_index_groups=ring)
     own = call(
         place_kernel,
@@ -300,21 +296,21 @@
     back = lax.ppermute(away, "tensor", swap)
     part = call(
         second_kernel,
-        shape((total, early), BF16),
-        [VMEM] * 2,
+        shape((total, width), BF16),
+        [VMEM] * 3,
         VMEM,
-        2 * total * early * units,
+        2 * total * width * units,
         4 * total * units,
-    )(hidden, w_second)
+    )(hidden, w_second, extra)
     return call(
         final_kernel,
         shape((total, width), BF16),
-        [VMEM] * 4,
+        [VMEM] * 3,
         ANY,
         total * width,
         4 * total * width,
-        [pltpu.VMEM((total, width), BF16), dma((early // TILE + 1,))],
-    )(part, extra, back, b_second.reshape(1, -1))
+        [pltpu.VMEM((total, width), BF16), dma((PIECES,))],
+    )(part, back, b_second.reshape(1, -1))
 
 
 def solution(mesh):

time: 33.8 us -> 33.3 us (0.985)
  Pallas kernels: 8.62 us -> 8.14 us
    pallas_call x1, Pallas kernels: 0.98 us -> 0.61 us  [shards(): call(pool_kernel, shape((groups, rows + NOTE, LANES), BF16), [VMEM] * 3,...]
where the time goes in v4:
time: 33.3 us; the launch traced here: 33.1 us
  blocking collectives  23.3 us (70%)
  Pallas kernels  8.14 us (24%)
  waiting for transfers between devices  1.22 us (4%)
    all_to_all x1, blocking collectives, shards(): lax.all_to_all(outgoing, 'dp', split_axis=0, concat_axis=0, tiled=True, a...  23.3 us
    pallas_call x1, Pallas kernels, shards(): call(hidden_kernel, (shape((total, units), BF16), shape((total, width), B...  2.85 us
    pallas_call x1, Pallas kernels, shards(): call(second_kernel, shape((total, width), BF16), [VMEM] * 3, VMEM, 2 * to...  1.42 us
    pallas_call x1, Pallas kernels, shards(): call(functools.partial(load_kernel, groups - lead), (pltpu.VMEM((groups *...  1.14 us
    pallas_call x1, Pallas kernels, shards(): call(final_kernel, shape((total, width), BF16), [VMEM] * 3, ANY, total *...  0.89 us
    pallas_call x1, Pallas kernels, shards(): call(first_kernel, shape((total, units), F32), [VMEM] * 2, VMEM, 2 * tota...  0.78 us
    ppermute x1, waiting for transfers between devices, shards(): other = lax.ppermute(own, 'tensor', swap)  0.77 us
  transfers between devices with their start and end apart: 2, of which 2 were waited for; matrix products, arithmetic and copies ran while one was open for 0% of the time, Pallas kernels for 7%

profile of v4, /device:TPU:0, one launch (start us, length us, event | category | flops | bytes accessed | tf_op | source)
XLA Modules:
  0.0 33.1 jit_solution(3687266310188603701)
XLA Ops:
  0.0 1.1 %load.1 = (bf16[512,512]{1,0:T(8,128)(2,1)S(1)}, bf16[16,8,128]{2,1,0:T(8,128)(2,1)S(1)}, bf16[576,512]{1,0:T(8,128)(2,1)S(1)}) custom-call(s32[8]{0:T(128)} %counts_in.1, s32[8]{0:T(128)} %seq_in.1, s32[8]{0:T(128)} %slot_in.1, s32[8,64]{1,0:T(8,128)} %win_in.1, bf16[576,512]{1,0:T(8,128)(2,1)} %bitcast.3), custom_call_target="tpu_custom_call" | custom-call | bytes 589824 | tf_op jit(solution)/shard_map/load/pallas_call | solution.py:253
  1.2 0.0 slice-start
  1.2 0.0 copy-start.1
  1.2 0.0 copy-start
  1.2 0.0 slice-start.1
  1.2 0.0 slice-start.2
  1.2 0.6 %pool.1 = bf16[16,152,128]{2,1,0:T(8,128)(2,1)S(1)} custom-call(bf16[512,512]{1,0:T(8,128)(2,1)S(1)} %get-tuple-element.11.hot, bf16[16,8,128]{2,1,0:T(8,128)(2,1)S(1)} %get-tuple-element.12.note, bf16[576,512]{1,0:T(8,128)(2,1)S(1)} %get-tuple-element.13.enc), custom_call_target="tpu_custom_call" | custom-call | flops 20000000000 | bytes 60000000 | tf_op jit(solution)/shard_map/pool/pallas_call | solution.py:262
  1.8 23.3 %all_to_all.5.came = bf16[16,152,128]{2,1,0:T(8,128)(2,1)S(1)} all-to-all(bf16[16,152,128]{2,1,0:T(8,128)(2,1)S(1)} %pool.1), channel_id=1, replica_groups={{22,24,26,28,30,0,2,4,6,8,10,12,14,16,18,20},{23,25,27,29,31,1,3,5,7,9,..., dimensions={0} | all-to-all | bytes 1245184 | tf_op jit(solution)/shard_map/all_to_all | solution.py:270
  25.1 0.4 %place.1.own = bf16[256,640]{1,0:T(8,128)(2,1)S(1)} custom-call(bf16[16,152,128]{2,1,0:T(8,128)(2,1)S(1)} %all_to_all.5.came), custom_call_target="tpu_custom_call" | custom-call | flops 150994944 | bytes 589824 | tf_op jit(solution)/shard_map/place/pallas_call | solution.py:271
  25.6 0.1 collective-permute-start
  25.6 0.0 copy-done.1
  25.7 0.0 copy-done
  25.7 0.8 %first.1.acc = f32[256,2304]{1,0:T(8,128)S(1)} custom-call(bf16[256,640]{1,0:T(8,128)(2,1)S(1)} %place.1.own, bf16[1152,2304]{1,0:T(8,128)(2,1)S(1)} %copy-done), custom_call_target="tpu_custom_call" | custom-call | flops 679477248 | bytes 2359296 | tf_op jit(solution)/shard_map/first/pallas_call | solution.py:280
  26.5 0.0 copy-start.2
  26.5 0.8 %collective-permute-done.other = bf16[256,640]{1,0:T(8,128)(2,1)S(1)} collective-permute-done((bf16[256,640]{1,0:T(8,128)(2,1)S(1)}, bf16[256,640]{1,0:T(8,128)(2,1)S(1)}, u32[]{:S(2)}, u32[]{:S(2)}) %collective-permute-start) | collective-permute-done | bytes 327712 | tf_op jit(solution)/shard_map/ppermute | solution.py:279
  27.3 0.0 slice-done
  27.3 0.0 slice-done.1
  27.3 0.0 slice-done.2
  27.3 2.9 %hidden.1 = (bf16[256,2304]{1,0:T(8,128)(2,1)S(1)}, bf16[256,1152]{1,0:T(8,128)(2,1)S(1)}, bf16[256,128]{1,0:T(8,128)(2,1)S(1)}) custom-call(f32[256,2304]{1,0:T(8,128)S(1)} %first.1.acc, bf16[256,640]{1,0:T(8,128)(2,1)S(1)} %place.1.own, bf16[256,640]{1,0:T(8,128)(2,1)S(1)} %collective-permute-done.other, bf16[1152,2304]{1,0:T(8,128)(2,1)S(1)} %copy-done, ...), custom_call_target="tpu_custom_call" | custom-call | flops 2038431744 | bytes 2359296 | tf_op jit(solution)/shard_map/hidden/pallas_call | solution.py:288
  30.1 0.2 collective-permute-start.1
  30.3 0.0 copy-done.2
  30.3 1.4 %second.1.part = bf16[256,1152]{1,0:T(8,128)(2,1)S(1)} custom-call(bf16[256,2304]{1,0:T(8,128)(2,1)S(1)} %get-tuple-element.14.hidden, bf16[2304,2304]{1,0:T(8,128)(2,1)S(1)} %bitcast.2, bf16[256,128]{1,0:T(8,128)(2,1)S(1)} %get-tuple-element.15.extra), custom_call_target="tpu_custom_call" | custom-call | flops 1358954496 | bytes 2359296 | tf_op jit(solution)/shard_map/second/pallas_call | solution.py:297
  31.8 0.4 %collective-permute-done.1.back = bf16[256,1152]{1,0:T(8,128)(2,1)S(1)} collective-permute-done((bf16[256,1152]{1,0:T(8,128)(2,1)S(1)}, bf16[256,1152]{1,0:T(8,128)(2,1)S(1)}, u32[]{:S(2)}, u32[]{:S(2)}) %collective-permute-start.1) | collective-permute-done | bytes 589856 | tf_op jit(solution)/shard_map/ppermute | solution.py:296
  32.2 0.9 %final.1 = bf16[256,1152]{1,0:T(8,128)(2,1)} custom-call(bf16[256,1152]{1,0:T(8,128)(2,1)S(1)} %second.1.part, bf16[256,1152]{1,0:T(8,128)(2,1)S(1)} %collective-permute-done.1.back, f32[1,1152]{1,0:T(1,128)S(1)} %reshape.7.b), custom_call_target="tpu_custom_call" | custom-call | flops 294912 | bytes 1179648 | tf_op jit(solution)/shard_map/final/pallas_call | solution.py:305
  (3 shorter events, 0.0 us)
Async XLA Ops:
  1.2 26.1 %slice-start = ((s8[10616832]{0:T(1024)(128)(4,1)}), s8[4194304]{0:T(1024)(128)(4,1)S(1)}, s32[]{:S(2)}) async-start(s8[10616832]{0:T(1024)(128)(4,1)} %bitcast.1), calls=%async_computation.1 | async-start | bytes 8388608
  1.2 24.5 %copy-start.1 = (f32[2304]{0:T(1024)S(1)}, f32[2304]{0:T(1024)}, u32[]{:S(2)}) copy-start(f32[2304]{0:T(1024)} %param.15) | copy-start | bytes 27652
  1.2 24.5 %copy-start = (bf16[1152,2304]{1,0:T(8,128)(2,1)S(1)}, bf16[1152,2304]{1,0:T(8,128)(2,1)}, u32[]{:S(2)}) copy-start(bf16[1152,2304]{1,0:T(8,128)(2,1)} %w.3) | copy-start | bytes 15925252
  1.2 26.1 %slice-start.1 = ((s8[10616832]{0:T(1024)(128)(4,1)}), s8[4194304]{0:T(1024)(128)(4,1)S(1)}, s32[]{:S(2)}) async-start(s8[10616832]{0:T(1024)(128)(4,1)} %bitcast.1), calls=%async_computation.2 | async-start | bytes 8388608
  1.2 26.1 %slice-start.2 = ((s8[10616832]{0:T(1024)(128)(4,1)}), s8[2228224]{0:T(1024)(128)(4,1)S(1)}, s32[]{:S(2)}) async-start(s8[10616832]{0:T(1024)(128)(4,1)} %bitcast.1), calls=%async_computation.3 | async-start | bytes 4456448
  25.6 1.7 %collective-permute-start = (bf16[256,640]{1,0:T(8,128)(2,1)S(1)}, bf16[256,640]{1,0:T(8,128)(2,1)S(1)}, u32[]{:S(2)}, u32[]{:S(2)}) collective-permute-start(bf16[256,640]{1,0:T(8,128)(2,1)S(1)} %place.1.own), channel_id=1, source_target_pairs={{0,1},{1,0},{2,3},{3,2},{4,5},{5,4},{6,7},{7,6},{8,9},{9,8},{10,11... | collective-permute-start | bytes 983048 | tf_op jit(solution)/shard_map/ppermute | solution.py:279
  26.5 3.9 %copy-start.2 = (f32[1152]{0:T(1024)S(1)}, f32[1152]{0:T(1024)}, u32[]{:S(2)}) copy-start(f32[1152]{0:T(1024)} %param.17) | copy-start | bytes 13828
  30.1 2.1 %collective-permute-start.1 = (bf16[256,1152]{1,0:T(8,128)(2,1)S(1)}, bf16[256,1152]{1,0:T(8,128)(2,1)S(1)}, u32[]{:S(2)}, u32[]{:S(2)}) collective-permute-start(bf16[256,1152]{1,0:T(8,128)(2,1)S(1)} %get-tuple-element.16), channel_id=1, source_target_pairs={{0,1},{1,0},{2,3},{3,2},{4,5},{5,4},{6,7},{7,6},{8,9},{9,8},{10,11... | collective-permute-start | bytes 1769480 | tf_op jit(solution)/shard_map/ppermute | solution.py:296

commit v5 on v4

--- a/solution.py
+++ b/solution.py
@@ -11,7 +11,7 @@
 BLOCK = 32
 LANES = 128
 HALF = LANES // 2
-NOTE = 8
+NOTE = 2
 F32, BF16, I32 = jnp.float32, jnp.bfloat16, jnp.int32
 VMEM = pl.BlockSpec(memory_space=pltpu.VMEM)
 SMEM = pl.BlockSpec(memory_space=pltpu.SMEM)
@@ -40,7 +40,7 @@
 def load_kernel(shift, counts_in, seq_in, slot_in, win_in, enc_in, hot, note, enc, counts, seq, slot, win, small, large):
     samples, cap = win.shape
     tokens = enc.shape[1]
-    groups = note.shape[0]
+    groups = note.shape[0] // NOTE
     smalls = [
         pltpu.make_async_copy(a, b, small.at[i])
         for i, (a, b) in enumerate(((win_in, win), (counts_in, counts), (seq_in, seq), (slot_in, slot)))
@@ -61,8 +61,8 @@
     owner, place = lane // cap, lane % cap
     live = jnp.zeros((1, tokens), I32)
     base = jnp.zeros((1, tokens), I32)
-    notes = jnp.zeros((groups, NOTE, LANES), I32)
-    target = iota((groups, NOTE, LANES), 0)
+    notes = jnp.zeros(note.shape, I32)
+    target = iota(note.shape, 0) // NOTE
     for n in range(samples):
         goal = seq[n] + shift
         goal = jnp.where(goal >= groups, goal - groups, goal)
@@ -79,12 +79,14 @@
 
 def pool_kernel(hot, note, enc, out):
     features, tokens = enc.shape
-    groups = out.shape[0]
     full, rest, rows = block_rows(features)
-    out[:, rows:, :] = note[...]
+    pitch = rows + NOTE
+    groups = out.shape[0] // pitch
     ones = jnp.ones((LANES, tokens), BF16)
     tail = enc[full * LANES :, :]
     tail = jnp.concatenate([tail, tail, ones] if rest else [ones], axis=0)
+    for g in range(groups):
+        out[g * pitch + rows : (g + 1) * pitch, :] = note[g * NOTE : (g + 1) * NOTE, :]
     per = min(groups, 16)
     for g in range(0, groups, per):
         pick = hot[g * BLOCK : (g + per) * BLOCK, :]
@@ -94,39 +96,47 @@
             got = (last[:, :LANES] * scale).reshape(per, BLOCK, LANES)
             low, high = got[:, : BLOCK // 2], got[:, BLOCK // 2 :]
             left = iota(low.shape, 2) < HALF
-            out[g : g + per, full * BLOCK : rows, :] = jnp.where(left, low, high).astype(BF16)
+            got = jnp.where(left, low, high).astype(BF16)
+            for i in range(per):
+                at = (g + i) * pitch + full * BLOCK
+                out[at : at + BLOCK // 2, :] = got[i]
         for c in range(0, full * LANES, TILE):
             n = min(TILE, full * LANES - c)
             both = lax.dot_general(pick, enc[c : c + n, :], NT, preferred_element_type=F32)
             for j in range(0, n, LANES):
-                got = (both[:, j : j + LANES] * scale).astype(BF16).reshape(per, BLOCK, LANES)
-                at = (c + j) // LANES * BLOCK
-                out[g : g + per, at : at + BLOCK, :] = got
-
-
-def place_kernel(came, out):
-    groups = came.shape[0]
+                got = (both[:, j : j + LANES] * scale).astype(BF16)
+                for i in range(per):
+                    at = (g + i) * pitch + (c + j) // LANES * BLOCK
+                    out[at : at + BLOCK, :] = got[i * BLOCK : (i + 1) * BLOCK]
+
+
+def place_kernel(came, out, *, groups):
     total, padded = out.shape
-    rows = came.shape[1] - NOTE
+    pitch = came.shape[0] // groups
+    rows = pitch - NOTE
     full = rows // BLOCK
     each = LANES // BLOCK
-    turn = iota((NOTE, LANES), 1) // BLOCK
+    turn = iota((1, LANES), 1) // BLOCK
     keys = []
     for d in range(0, groups, each):
-        key = came[d, rows:, :].astype(F32)
+        ends = [came[(d + i) * pitch + rows : (d + i + 1) * pitch, :].astype(F32)[:1] for i in range(each)]
+        key = ends[0]
         for i in range(1, each):
-            key = jnp.where(turn == i, came[d + i, rows:, :].astype(F32), key)
+            key = jnp.where(turn == i, ends[i], key)
         keys.append(key)
-    key = jnp.concatenate(keys, axis=1)[:1].astype(I32)
+    key = jnp.concatenate(keys, axis=1).astype(I32)
     key = (key - 1) * BLOCK + iota((1, groups * BLOCK), 1) % BLOCK
     hot = (iota((total, groups * BLOCK), 0) == key).astype(F32).astype(BF16)
+
+    def strip(first, size):
+        return [came[d * pitch + first : d * pitch + first + size, :] for d in range(groups)]
+
     for j in range(0, full, 2):
-        parts = [came[:, i * BLOCK : (i + 1) * BLOCK, :].reshape(groups * BLOCK, LANES) for i in range(j, min(j + 2, full))]
+        parts = [jnp.concatenate(strip(i * BLOCK, BLOCK), axis=0) for i in range(j, min(j + 2, full))]
         got = jnp.dot(hot, jnp.concatenate(parts, axis=1), preferred_element_type=F32)
         out[:, j * LANES : (j + len(parts)) * LANES] = got.astype(BF16)
     if rows > full * BLOCK:
-        part = came[:, full * BLOCK : rows, :]
-        twice = jnp.concatenate([part, part], axis=1).reshape(groups * BLOCK, LANES)
+        twice = jnp.concatenate([x for part in strip(full * BLOCK, BLOCK // 2) for x in (part, part)], axis=0)
         got = jnp.dot(hot, twice, preferred_element_type=F32)
         low = iota((total, LANES), 0) % BLOCK < BLOCK // 2
         left = iota((total, LANES), 1) < HALF
@@ -252,7 +262,7 @@
 
     hot, note, enc = call(
         functools.partial(load_kernel, groups - lead),
-        (pltpu.VMEM((groups * BLOCK, tokens), BF16), pltpu.VMEM((groups, NOTE, LANES), BF16), pltpu.VMEM((features, tokens), BF16)),
+        (pltpu.VMEM((groups * BLOCK, tokens), BF16), pltpu.VMEM((groups * NOTE, LANES), BF16), pltpu.VMEM((features, tokens), BF16)),
         [HBM] * 5,
         (VMEM, VMEM, VMEM),
         0,
@@ -261,15 +271,17 @@
     )(in_hbm(counts), in_hbm(dest_seq), in_hbm(dest_slot), in_hbm(win_ids), in_hbm(encoded.T))
     outgoing = call(
         pool_kernel,
-        shape((groups, rows + NOTE, LANES), BF16),
+        shape((groups * (rows + NOTE), LANES), BF16),
         [VMEM] * 3,
         VMEM,
         POOL_FLOPS,
         POOL_BYTES,
     )(hot, note, enc)
+    outgoing = outgoing.reshape(groups, -1, NOTE, LANES)
     came = lax.all_to_all(outgoing, "dp", split_axis=0, concat_axis=0, tiled=True, axis_index_groups=ring)
+    came = came.reshape(-1, LANES)
     own = call(
-        place_kernel,
+        functools.partial(place_kernel, groups=groups),
         shape((total, (full + (rest > 0)) * LANES), BF16),
         [VMEM],
         VMEM,

time: 33.3 us -> 32.9 us (0.988)
  blocking collectives: 23.3 us -> 22.8 us
    all_to_all x1, blocking collectives: 23.3 us -> 22.8 us  [shards(): lax.all_to_all(outgoing, 'dp', split_axis=0, concat_axis=0, tiled=True, a...]
where the time goes in v5:
time: 32.9 us; the launch traced here: 32.7 us
  blocking collectives  22.8 us (69%)
  Pallas kernels  8.19 us (25%)
  waiting for transfers between devices  1.22 us (4%)
    all_to_all x1, blocking collectives, shards(): lax.all_to_all(outgoing, 'dp', split_axis=0, concat_axis=0, tiled=True, a...  22.8 us
    pallas_call x1, Pallas kernels, shards(): call(hidden_kernel, (shape((total, units), BF16), shape((total, width), B...  2.85 us
    pallas_call x1, Pallas kernels, shards(): call(second_kernel, shape((total, width), BF16), [VMEM] * 3, VMEM, 2 * to...  1.42 us
    pallas_call x1, Pallas kernels, shards(): call(functools.partial(load_kernel, groups - lead), (pltpu.VMEM((groups *...  1.14 us
    pallas_call x1, Pallas kernels, shards(): call(final_kernel, shape((total, width), BF16), [VMEM] * 3, ANY, total *...  0.89 us
    pallas_call x1, Pallas kernels, shards(): call(first_kernel, shape((total, units), F32), [VMEM] * 2, VMEM, 2 * tota...  0.78 us
    ppermute x1, waiting for transfers between devices, shards(): other = lax.ppermute(own, 'tensor', swap)  0.77 us
  transfers between devices with their start and end apart: 2, of which 2 were waited for; matrix products, arithmetic and copies ran while one was open for 0% of the time, Pallas kernels for 7%

profile of v5, /device:TPU:0, one launch (start us, length us, event | category | flops | bytes accessed | tf_op | source)
XLA Modules:
  0.0 32.7 jit_solution(13507447590851389445)
XLA Ops:
  0.0 1.1 %load.1 = (bf16[512,512]{1,0:T(8,128)(2,1)S(1)}, bf16[32,128]{1,0:T(8,128)(2,1)S(1)}, bf16[576,512]{1,0:T(8,128)(2,1)S(1)}) custom-call(s32[8]{0:T(128)} %counts_in.1, s32[8]{0:T(128)} %seq_in.1, s32[8]{0:T(128)} %slot_in.1, s32[8,64]{1,0:T(8,128)} %win_in.1, bf16[576,512]{1,0:T(8,128)(2,1)} %bitcast.7), custom_call_target="tpu_custom_call" | custom-call | bytes 589824 | tf_op jit(solution)/shard_map/load/pallas_call | solution.py:263
  1.2 0.0 slice-start
  1.2 0.0 copy-start.1
  1.2 0.0 copy-start
  1.2 0.0 slice-start.1
  1.2 0.0 slice-start.2
  1.2 0.6 %pool.1 = bf16[2336,128]{1,0:T(8,128)(2,1)S(1)} custom-call(bf16[512,512]{1,0:T(8,128)(2,1)S(1)} %get-tuple-element.11.hot, bf16[32,128]{1,0:T(8,128)(2,1)S(1)} %get-tuple-element.12.note, bf16[576,512]{1,0:T(8,128)(2,1)S(1)} %get-tuple-element.13.enc), custom_call_target="tpu_custom_call" | custom-call | flops 20000000000 | bytes 60000000 | tf_op jit(solution)/shard_map/pool/pallas_call | solution.py:272
  1.9 22.8 %all_to_all.5 = bf16[16,73,2,128]{3,2,1,0:T(2,128)(2,1)S(1)} all-to-all(bf16[16,73,2,128]{3,2,1,0:T(2,128)(2,1)S(1)} %bitcast.6), channel_id=1, replica_groups={{22,24,26,28,30,0,2,4,6,8,10,12,14,16,18,20},{23,25,27,29,31,1,3,5,7,9,..., dimensions={0} | all-to-all | bytes 1196032 | tf_op jit(solution)/shard_map/all_to_all | solution.py:281
  24.7 0.5 %place.1.own = bf16[256,640]{1,0:T(8,128)(2,1)S(1)} custom-call(bf16[2336,128]{1,0:T(8,128)(2,1)S(1)} %bitcast.5), custom_call_target="tpu_custom_call" | custom-call | flops 150994944 | bytes 589824 | tf_op jit(solution)/shard_map/place/pallas_call | solution.py:283
  25.1 0.1 collective-permute-start
  25.2 0.0 copy-done.1
  25.2 0.0 copy-done
  25.2 0.8 %first.1.acc = f32[256,2304]{1,0:T(8,128)S(1)} custom-call(bf16[256,640]{1,0:T(8,128)(2,1)S(1)} %place.1.own, bf16[1152,2304]{1,0:T(8,128)(2,1)S(1)} %copy-done), custom_call_target="tpu_custom_call" | custom-call | flops 679477248 | bytes 2359296 | tf_op jit(solution)/shard_map/first/pallas_call | solution.py:292
  26.0 0.0 copy-start.2
  26.1 0.8 %collective-permute-done.other = bf16[256,640]{1,0:T(8,128)(2,1)S(1)} collective-permute-done((bf16[256,640]{1,0:T(8,128)(2,1)S(1)}, bf16[256,640]{1,0:T(8,128)(2,1)S(1)}, u32[]{:S(2)}, u32[]{:S(2)}) %collective-permute-start) | collective-permute-done | bytes 327712 | tf_op jit(solution)/shard_map/ppermute | solution.py:291
  26.8 0.0 slice-done
  26.8 0.0 slice-done.1
  26.8 0.0 slice-done.2
  26.8 2.8 %hidden.1 = (bf16[256,2304]{1,0:T(8,128)(2,1)S(1)}, bf16[256,1152]{1,0:T(8,128)(2,1)S(1)}, bf16[256,128]{1,0:T(8,128)(2,1)S(1)}) custom-call(f32[256,2304]{1,0:T(8,128)S(1)} %first.1.acc, bf16[256,640]{1,0:T(8,128)(2,1)S(1)} %place.1.own, bf16[256,640]{1,0:T(8,128)(2,1)S(1)} %collective-permute-done.other, bf16[1152,2304]{1,0:T(8,128)(2,1)S(1)} %copy-done, ...), custom_call_target="tpu_custom_call" | custom-call | flops 2038431744 | bytes 2359296 | tf_op jit(solution)/shard_map/hidden/pallas_call | solution.py:300
  29.7 0.2 collective-permute-start.1
  29.9 0.0 copy-done.2
  29.9 1.4 %second.1.part = bf16[256,1152]{1,0:T(8,128)(2,1)S(1)} custom-call(bf16[256,2304]{1,0:T(8,128)(2,1)S(1)} %get-tuple-element.14.hidden, bf16[2304,2304]{1,0:T(8,128)(2,1)S(1)} %bitcast.4, bf16[256,128]{1,0:T(8,128)(2,1)S(1)} %get-tuple-element.15.extra), custom_call_target="tpu_custom_call" | custom-call | flops 1358954496 | bytes 2359296 | tf_op jit(solution)/shard_map/second/pallas_call | solution.py:309
  31.3 0.4 %collective-permute-done.1.back = bf16[256,1152]{1,0:T(8,128)(2,1)S(1)} collective-permute-done((bf16[256,1152]{1,0:T(8,128)(2,1)S(1)}, bf16[256,1152]{1,0:T(8,128)(2,1)S(1)}, u32[]{:S(2)}, u32[]{:S(2)}) %collective-permute-start.1) | collective-permute-done | bytes 589856 | tf_op jit(solution)/shard_map/ppermute | solution.py:308
  31.8 0.9 %final.1 = bf16[256,1152]{1,0:T(8,128)(2,1)} custom-call(bf16[256,1152]{1,0:T(8,128)(2,1)S(1)} %second.1.part, bf16[256,1152]{1,0:T(8,128)(2,1)S(1)} %collective-permute-done.1.back, f32[1,1152]{1,0:T(1,128)S(1)} %reshape.15.b), custom_call_target="tpu_custom_call" | custom-call | flops 294912 | bytes 1179648 | tf_op jit(solution)/shard_map/final/pallas_call | solution.py:317
  (3 shorter events, 0.0 us)
Async XLA Ops:
  1.2 25.7 %slice-start = ((s8[10616832]{0:T(1024)(128)(4,1)}), s8[4194304]{0:T(1024)(128)(4,1)S(1)}, s32[]{:S(2)}) async-start(s8[10616832]{0:T(1024)(128)(4,1)} %bitcast.3), calls=%async_computation.1 | async-start | bytes 8388608
  1.2 24.0 %copy-start.1 = (f32[2304]{0:T(1024)S(1)}, f32[2304]{0:T(1024)}, u32[]{:S(2)}) copy-start(f32[2304]{0:T(1024)} %param.15) | copy-start | bytes 27652
  1.2 24.1 %copy-start = (bf16[1152,2304]{1,0:T(8,128)(2,1)S(1)}, bf16[1152,2304]{1,0:T(8,128)(2,1)}, u32[]{:S(2)}) copy-start(bf16[1152,2304]{1,0:T(8,128)(2,1)} %w.3) | copy-start | bytes 15925252
  1.2 25.6 %slice-start.1 = ((s8[10616832]{0:T(1024)(128)(4,1)}), s8[4194304]{0:T(1024)(128)(4,1)S(1)}, s32[]{:S(2)}) async-start(s8[10616832]{0:T(1024)(128)(4,1)} %bitcast.3), calls=%async_computation.2 | async-start | bytes 8388608
  1.2 25.6 %slice-start.2 = ((s8[10616832]{0:T(1024)(128)(4,1)}), s8[2228224]{0:T(1024)(128)(4,1)S(1)}, s32[]{:S(2)}) async-start(s8[10616832]{0:T(1024)(128)(4,1)} %bitcast.3), calls=%async_computation.3 | async-start | bytes 4456448
  25.1 1.7 %collective-permute-start = (bf16[256,640]{1,0:T(8,128)(2,1)S(1)}, bf16[256,640]{1,0:T(8,128)(2,1)S(1)}, u32[]{:S(2)}, u32[]{:S(2)}) collective-permute-start(bf16[256,640]{1,0:T(8,128)(2,1)S(1)} %place.1.own), channel_id=1, source_target_pairs={{0,1},{1,0},{2,3},{3,2},{4,5},{5,4},{6,7},{7,6},{8,9},{9,8},{10,11... | collective-permute-start | bytes 983048 | tf_op jit(solution)/shard_map/ppermute | solution.py:291
  26.0 3.9 %copy-start.2 = (f32[1152]{0:T(1024)S(1)}, f32[1152]{0:T(1024)}, u32[]{:S(2)}) copy-start(f32[1152]{0:T(1024)} %param.17) | copy-start | bytes 13828
  29.7 2.1 %collective-permute-start.1 = (bf16[256,1152]{1,0:T(8,128)(2,1)S(1)}, bf16[256,1152]{1,0:T(8,128)(2,1)S(1)}, u32[]{:S(2)}, u32[]{:S(2)}) collective-permute-start(bf16[256,1152]{1,0:T(8,128)(2,1)S(1)} %get-tuple-element.16), channel_id=1, source_target_pairs={{0,1},{1,0},{2,3},{3,2},{4,5},{5,4},{6,7},{7,6},{8,9},{9,8},{10,11... | collective-permute-start | bytes 1769480 | tf_op jit(solution)/shard_map/ppermute | solution.py:308

commit v6 on v5

--- a/solution.py
+++ b/solution.py
@@ -19,7 +19,7 @@
 HBM = pl.BlockSpec(memory_space=pltpu.HBM)
 NT = (((1,), (1,)), ((), ()))
 TILE = 256
-PIECES = 4
+PIECES = 8
 GRANT = 20 << 20
 POOL_FLOPS, POOL_BYTES = 2e10, 6e7
 GELU_A = (2 / math.pi) ** 0.5

time: 32.9 us -> 32.9 us (level)
  no operation moved by 1% of the time
where the time goes in v6:
time: 32.9 us; the launch traced here: 32.7 us
  blocking collectives  22.8 us (69%)
  Pallas kernels  8.2 us (25%)
  waiting for transfers between devices  1.22 us (4%)
    all_to_all x1, blocking collectives, shards(): lax.all_to_all(outgoing, 'dp', split_axis=0, concat_axis=0, tiled=True, a...  22.8 us
    pallas_call x1, Pallas kernels, shards(): call(hidden_kernel, (shape((total, units), BF16), shape((total, width), B...  2.85 us
    pallas_call x1, Pallas kernels, shards(): call(second_kernel, shape((total, width), BF16), [VMEM] * 3, VMEM, 2 * to...  1.42 us
    pallas_call x1, Pallas kernels, shards(): call(functools.partial(load_kernel, groups - lead), (pltpu.VMEM((groups *...  1.14 us
    pallas_call x1, Pallas kernels, shards(): call(final_kernel, shape((total, width), BF16), [VMEM] * 3, ANY, total *...  0.9 us
    pallas_call x1, Pallas kernels, shards(): call(first_kernel, shape((total, units), F32), [VMEM] * 2, VMEM, 2 * tota...  0.78 us
    ppermute x1, waiting for transfers between devices, shards(): other = lax.ppermute(own, 'tensor', swap)  0.77 us
  transfers between devices with their start and end apart: 2, of which 2 were waited for; matrix products, arithmetic and copies ran while one was open for 0% of the time, Pallas kernels for 7%

profile of v6, /device:TPU:0, one launch (start us, length us, event | category | flops | bytes accessed | tf_op | source)
XLA Modules:
  0.0 32.7 jit_solution(595505833211578250)
XLA Ops:
  0.0 1.1 %load.1 = (bf16[512,512]{1,0:T(8,128)(2,1)S(1)}, bf16[32,128]{1,0:T(8,128)(2,1)S(1)}, bf16[576,512]{1,0:T(8,128)(2,1)S(1)}) custom-call(s32[8]{0:T(128)} %counts_in.1, s32[8]{0:T(128)} %seq_in.1, s32[8]{0:T(128)} %slot_in.1, s32[8,64]{1,0:T(8,128)} %win_in.1, bf16[576,512]{1,0:T(8,128)(2,1)} %bitcast.7), custom_call_target="tpu_custom_call" | custom-call | bytes 589824 | tf_op jit(solution)/shard_map/load/pallas_call | solution.py:263
  1.2 0.0 slice-start
  1.2 0.0 copy-start.1
  1.2 0.0 copy-start
  1.2 0.0 slice-start.1
  1.2 0.0 slice-start.2
  1.2 0.6 %pool.1 = bf16[2336,128]{1,0:T(8,128)(2,1)S(1)} custom-call(bf16[512,512]{1,0:T(8,128)(2,1)S(1)} %get-tuple-element.11.hot, bf16[32,128]{1,0:T(8,128)(2,1)S(1)} %get-tuple-element.12.note, bf16[576,512]{1,0:T(8,128)(2,1)S(1)} %get-tuple-element.13.enc), custom_call_target="tpu_custom_call" | custom-call | flops 20000000000 | bytes 60000000 | tf_op jit(solution)/shard_map/pool/pallas_call | solution.py:272
  1.9 22.8 %all_to_all.5 = bf16[16,73,2,128]{3,2,1,0:T(2,128)(2,1)S(1)} all-to-all(bf16[16,73,2,128]{3,2,1,0:T(2,128)(2,1)S(1)} %bitcast.6), channel_id=1, replica_groups={{22,24,26,28,30,0,2,4,6,8,10,12,14,16,18,20},{23,25,27,29,31,1,3,5,7,9,..., dimensions={0} | all-to-all | bytes 1196032 | tf_op jit(solution)/shard_map/all_to_all | solution.py:281
  24.7 0.5 %place.1.own = bf16[256,640]{1,0:T(8,128)(2,1)S(1)} custom-call(bf16[2336,128]{1,0:T(8,128)(2,1)S(1)} %bitcast.5), custom_call_target="tpu_custom_call" | custom-call | flops 150994944 | bytes 589824 | tf_op jit(solution)/shard_map/place/pallas_call | solution.py:283
  25.1 0.1 collective-permute-start
  25.2 0.0 copy-done.1
  25.2 0.0 copy-done
  25.2 0.8 %first.1.acc = f32[256,2304]{1,0:T(8,128)S(1)} custom-call(bf16[256,640]{1,0:T(8,128)(2,1)S(1)} %place.1.own, bf16[1152,2304]{1,0:T(8,128)(2,1)S(1)} %copy-done), custom_call_target="tpu_custom_call" | custom-call | flops 679477248 | bytes 2359296 | tf_op jit(solution)/shard_map/first/pallas_call | solution.py:292
  26.0 0.0 copy-start.2
  26.1 0.8 %collective-permute-done.other = bf16[256,640]{1,0:T(8,128)(2,1)S(1)} collective-permute-done((bf16[256,640]{1,0:T(8,128)(2,1)S(1)}, bf16[256,640]{1,0:T(8,128)(2,1)S(1)}, u32[]{:S(2)}, u32[]{:S(2)}) %collective-permute-start) | collective-permute-done | bytes 327712 | tf_op jit(solution)/shard_map/ppermute | solution.py:291
  26.8 0.0 slice-done
  26.8 0.0 slice-done.1
  26.8 0.0 slice-done.2
  26.8 2.8 %hidden.1 = (bf16[256,2304]{1,0:T(8,128)(2,1)S(1)}, bf16[256,1152]{1,0:T(8,128)(2,1)S(1)}, bf16[256,128]{1,0:T(8,128)(2,1)S(1)}) custom-call(f32[256,2304]{1,0:T(8,128)S(1)} %first.1.acc, bf16[256,640]{1,0:T(8,128)(2,1)S(1)} %place.1.own, bf16[256,640]{1,0:T(8,128)(2,1)S(1)} %collective-permute-done.other, bf16[1152,2304]{1,0:T(8,128)(2,1)S(1)} %copy-done, ...), custom_call_target="tpu_custom_call" | custom-call | flops 2038431744 | bytes 2359296 | tf_op jit(solution)/shard_map/hidden/pallas_call | solution.py:300
  29.7 0.2 collective-permute-start.1
  29.9 0.0 copy-done.2
  29.9 1.4 %second.1.part = bf16[256,1152]{1,0:T(8,128)(2,1)S(1)} custom-call(bf16[256,2304]{1,0:T(8,128)(2,1)S(1)} %get-tuple-element.14.hidden, bf16[2304,2304]{1,0:T(8,128)(2,1)S(1)} %bitcast.4, bf16[256,128]{1,0:T(8,128)(2,1)S(1)} %get-tuple-element.15.extra), custom_call_target="tpu_custom_call" | custom-call | flops 1358954496 | bytes 2359296 | tf_op jit(solution)/shard_map/second/pallas_call | solution.py:309
  31.3 0.4 %collective-permute-done.1.back = bf16[256,1152]{1,0:T(8,128)(2,1)S(1)} collective-permute-done((bf16[256,1152]{1,0:T(8,128)(2,1)S(1)}, bf16[256,1152]{1,0:T(8,128)(2,1)S(1)}, u32[]{:S(2)}, u32[]{:S(2)}) %collective-permute-start.1) | collective-permute-done | bytes 589856 | tf_op jit(solution)/shard_map/ppermute | solution.py:308
  31.8 0.9 %final.1 = bf16[256,1152]{1,0:T(8,128)(2,1)} custom-call(bf16[256,1152]{1,0:T(8,128)(2,1)S(1)} %second.1.part, bf16[256,1152]{1,0:T(8,128)(2,1)S(1)} %collective-permute-done.1.back, f32[1,1152]{1,0:T(1,128)S(1)} %reshape.15.b), custom_call_target="tpu_custom_call" | custom-call | flops 294912 | bytes 1179648 | tf_op jit(solution)/shard_map/final/pallas_call | solution.py:317
  (3 shorter events, 0.0 us)
Async XLA Ops:
  1.2 25.7 %slice-start = ((s8[10616832]{0:T(1024)(128)(4,1)}), s8[4194304]{0:T(1024)(128)(4,1)S(1)}, s32[]{:S(2)}) async-start(s8[10616832]{0:T(1024)(128)(4,1)} %bitcast.3), calls=%async_computation.1 | async-start | bytes 8388608
  1.2 24.0 %copy-start.1 = (f32[2304]{0:T(1024)S(1)}, f32[2304]{0:T(1024)}, u32[]{:S(2)}) copy-start(f32[2304]{0:T(1024)} %param.15) | copy-start | bytes 27652
  1.2 24.1 %copy-start = (bf16[1152,2304]{1,0:T(8,128)(2,1)S(1)}, bf16[1152,2304]{1,0:T(8,128)(2,1)}, u32[]{:S(2)}) copy-start(bf16[1152,2304]{1,0:T(8,128)(2,1)} %w.3) | copy-start | bytes 15925252
  1.2 25.6 %slice-start.1 = ((s8[10616832]{0:T(1024)(128)(4,1)}), s8[4194304]{0:T(1024)(128)(4,1)S(1)}, s32[]{:S(2)}) async-start(s8[10616832]{0:T(1024)(128)(4,1)} %bitcast.3), calls=%async_computation.2 | async-start | bytes 8388608
  1.2 25.6 %slice-start.2 = ((s8[10616832]{0:T(1024)(128)(4,1)}), s8[2228224]{0:T(1024)(128)(4,1)S(1)}, s32[]{:S(2)}) async-start(s8[10616832]{0:T(1024)(128)(4,1)} %bitcast.3), calls=%async_computation.3 | async-start | bytes 4456448
  25.1 1.7 %collective-permute-start = (bf16[256,640]{1,0:T(8,128)(2,1)S(1)}, bf16[256,640]{1,0:T(8,128)(2,1)S(1)}, u32[]{:S(2)}, u32[]{:S(2)}) collective-permute-start(bf16[256,640]{1,0:T(8,128)(2,1)S(1)} %place.1.own), channel_id=1, source_target_pairs={{0,1},{1,0},{2,3},{3,2},{4,5},{5,4},{6,7},{7,6},{8,9},{9,8},{10,11... | collective-permute-start | bytes 983048 | tf_op jit(solution)/shard_map/ppermute | solution.py:291
  26.0 3.9 %copy-start.2 = (f32[1152]{0:T(1024)S(1)}, f32[1152]{0:T(1024)}, u32[]{:S(2)}) copy-start(f32[1152]{0:T(1024)} %param.17) | copy-start | bytes 13828
  29.7 2.1 %collective-permute-start.1 = (bf16[256,1152]{1,0:T(8,128)(2,1)S(1)}, bf16[256,1152]{1,0:T(8,128)(2,1)S(1)}, u32[]{:S(2)}, u32[]{:S(2)}) collective-permute-start(bf16[256,1152]{1,0:T(8,128)(2,1)S(1)} %get-tuple-element.16), channel_id=1, source_target_pairs={{0,1},{1,0},{2,3},{3,2},{4,5},{5,4},{6,7},{7,6},{8,9},{9,8},{10,11... | collective-permute-start | bytes 1769480 | tf_op jit(solution)/shard_map/ppermute | solution.py:308
